TPU v7x, 512 devices: a whole 4x8x8 slice. The times are simulated.
512 devices in a mesh: cons: 16 (over y, x_lo), blk: 32 (over x_hi, z, core).
Axes of the slice: x: 4 (x_hi: 2, x_lo: 2; x = x_hi * 2 + x_lo), y: 8, z: 8, core: 2. Of those that a mesh axis runs over, the one named last changes fastest.
Arguments:
- elevation: bfloat16 [16, 1280, 6144], P('cons', 'blk'), may hold values from -6 to 6
- legendre: bfloat16 [1280, 768, 768], P('blk', 'cons'), may hold values from -5 to 5, as said below
- cycle_weight: float32 [1280], P('blk'), may hold values from 0.0001782951 to 0.0014263608
- love_factor: float32 [768], replicated, may hold values from 0.000390625 to 0.0052083335
- assignment: int32 [16], replicated, may hold values from 0 to 15, each once
Outputs:
- loading: float32 [16, 1280, 6144], P('cons', 'blk')
Inputs may be any that keep to these rules, and one draw needn't show every extreme that they name: `legendre`: fully normalized associated Legendre functions (the square integrates to 1 over [-1, 1]) of each cycle's latitude, every cycle within 26 degrees of the equator; zero where the degree is below the order.
All inputs are finite; a program needn't handle non-finite values.
Results may differ from a plain program's by a relative error of at most 0.02.
Values may be sent and summed in bfloat16 or wider, within the bound.
A program may use at most 128 MiB of HBM per device.

v0:
```python
import jax
import jax.numpy as jnp
from jax import lax
from jax.sharding import Mesh
from jax.sharding import PartitionSpec as P

BLK = ("blk_0", "blk_1", "blk_2")


def filled_up(lines, length):
    spare = -lines.shape[0] % length
    if not spare:
        return lines
    return jnp.concatenate([lines, jnp.zeros((spare, *lines.shape[1:]), lines.dtype)])


def from_everyone(array, axis):
    copies = jnp.broadcast_to(array, (lax.axis_size(axis), *array.shape))
    return lax.all_to_all(copies, axis, split_axis=0, concat_axis=0, tiled=True)


def joined_along(tiles, dim):
    dims = list(tiles.shape[1:])
    dims[dim] *= tiles.shape[0]
    return jnp.moveaxis(tiles, 0, dim).reshape(dims)


def gathered_by_axis(array, axes, dim):
    far, near = axes
    tiles = from_everyone(from_everyone(array, far), near)
    return joined_along(tiles.swapaxes(0, 1).reshape(-1, *array.shape), dim)


def in_blocks(array, dim, length):
    dims = array.shape
    tiles = array.reshape(*dims[:dim], length, dims[dim] // length, *dims[dim + 1 :])
    return jnp.moveaxis(tiles, dim, 0)


def sent_and_summed(array, axis, dim):
    length = lax.axis_size(axis)
    tiles = lax.all_to_all(in_blocks(array, dim, length), axis, 0, 0, tiled=True)
    return jnp.sum(tiles.astype(jnp.float32), axis=0)


def summed_rows(array, axes, dim):
    far, near = axes
    tiles = in_blocks(array, dim, lax.axis_size(far))
    nearer = sent_and_summed(tiles, near, dim + 1)
    arrived = lax.all_to_all(
        nearer.astype(jnp.bfloat16), far, split_axis=0, concat_axis=0, tiled=True
    )
    return arrived.astype(jnp.float32).sum(axis=0)


def sum_by_parts(array, axes):
    lines = array.reshape(-1, array.shape[-1])
    padded = filled_up(lines, lax.axis_size(axes[0]) * lax.axis_size(axes[1]))
    whole = gathered_by_axis(summed_rows(padded, axes, 0).astype(jnp.bfloat16), axes, 0)
    return lax.slice_in_dim(whole, 0, len(lines)).reshape(array.shape).astype(jnp.float32)


def fourier_halves(offset, length, period, orders):
    lon_index = offset + jnp.arange(length, dtype=jnp.int32)
    order_index = jnp.arange(orders, dtype=jnp.int32)
    phases = lon_index[:, None] * order_index[None, :] % period
    angles = phases.astype(jnp.float32) * jnp.float32(2.0 * 3.141592653589793 / period)
    cosine = jnp.cos(angles).astype(jnp.bfloat16)
    minus_sine = (-jnp.sin(angles)).astype(jnp.bfloat16)
    return jnp.stack([cosine, minus_sine], axis=1)


def local(elevation, legendre, cycle_weight, love_factor, assignment):
    fld_dev, cycle_dev, longitudes = elevation.shape
    orders_dev = legendre.shape[1]
    orders = orders_dev * lax.axis_size("cons")
    quarter_len = longitudes // 4
    table = jnp.concatenate(
        [
            fourier_halves(quarter * quarter_len, quarter_len, longitudes, orders)
            for quarter in range(4)
        ],
        axis=0,
    )
    running = jnp.einsum("fjk,kpm->fjpm", elevation, table, preferred_element_type=jnp.float32)
    spectra = (running * cycle_weight[None, :, None, None]).astype(jnp.bfloat16)
    moved = lax.all_to_all(spectra, "cons", split_axis=3, concat_axis=0, tiled=True)
    fields = moved.shape[0]
    one_hot = (assignment[:, None] == jnp.arange(fields, dtype=jnp.int32)[None, :]).astype(
        jnp.bfloat16
    )
    ordered = jnp.einsum(
        "gf,fjpm->gjpm", one_hot, moved, preferred_element_type=jnp.float32
    ).astype(jnp.bfloat16)
    whole = sum_by_parts(
        jnp.einsum("jml,gjpm->lpgm", legendre, ordered, preferred_element_type=jnp.float32).astype(
            jnp.bfloat16
        ),
        (("blk_0", "blk_1"), "blk_2"),
    )
    coefficients = (whole * love_factor[:, None, None, None]).astype(jnp.bfloat16)
    order_index = lax.axis_index("cons") * orders_dev + jnp.arange(orders_dev, dtype=jnp.int32)
    order_factor = jnp.where(order_index == 0, 1.0, 2.0).astype(jnp.float32)
    summed = jnp.einsum(
        "jml,lpgm->gjpm", legendre, coefficients, preferred_element_type=jnp.float32
    )
    synthesis = (summed * order_factor[None, None, None, :]).astype(jnp.bfloat16)
    returned = lax.all_to_all(synthesis, "cons", split_axis=0, concat_axis=3, tiled=True)
    return jnp.einsum("fjpm,kpm->fjk", returned, table, preferred_element_type=jnp.float32)


def solution(mesh):
    torus = Mesh(
        mesh.devices.reshape(mesh.shape["cons"], 2, 8, 2), ("cons", "blk_0", "blk_1", "blk_2")
    )
    placed = (P("cons", BLK, None), P(BLK, "cons", None), P(BLK), P(), P())
    return jax.shard_map(
        local, mesh=torus, in_specs=placed, out_specs=P("cons", BLK, None), check_vma=False
    )
```

profile of v0, /device:TPU:1, one launch (start us, length us, event | category | flops | bytes accessed | tf_op | source)
XLA Modules:
  0.0 338.6 jit_solution(15464694889144117104)
XLA Ops:
  0.0 18.9 %cosine_convert_fusion.3 = bf16[1536,1,768]{2,0,1:T(8,128)(2,1)} fusion(), kind=kLoop, calls=%fused_computation.32 | loop fusion | flops 11796480 | bytes 2359296 | tf_op jit(solution)/shard_map/convert_element_type | solution.py:68
  19.0 40.5 %cosine_convert_fusion.2 = (bf16[1536,1,768]{2,0,1:T(8,128)(2,1)}, bf16[1536,1,768]{2,0,1:T(8,128)(2,1)}, bf16[1536,1,768]{2,0,1:T(8,128)(2,1)}) fusion(s32[1536]{0:T(1024)S(1)} %iota_add_fusion.2), kind=kLoop, calls=%fused_computation.27 | loop fusion | flops 27131904 | bytes 7084032 | tf_op jit(solution)/shard_map/convert_element_type | solution.py:68
  59.4 42.6 %cosine_convert_fusion = (bf16[1536,1,768]{2,0,1:T(8,128)(2,1)}, bf16[1536,1,768]{2,0,1:T(8,128)(2,1)}, bf16[1536,1,768]{2,0,1:T(8,128)(2,1)}, bf16[1536,1,768]{2,0,1:T(8,128)(2,1)}) fusion(s32[1536]{0:T(1024)S(1)} %iota_add_fusion, s32[1536]{0:T(1024)S(1)} %iota_add_fusion.1), kind=kLoop, calls=%fused_computation.17 | loop fusion | flops 28311552 | bytes 9449472 | tf_op jit(solution)/shard_map/convert_element_type | solution.py:68
  102.0 21.5 %maximum_maximum_fusion = bf16[6144,2,768]{2,0,1:T(8,128)(2,1)} fusion(bf16[1536,1,768]{2,0,1:T(8,128)(2,1)} %get-tuple-element.10, bf16[1536,1,768]{2,0,1:T(8,128)(2,1)} %get-tuple-element.9, bf16[1536,1,768]{2,0,1:T(8,128)(2,1)} %get-tuple-element.11, bf16[1536,1,768]{2,0,1:T(8,128)(2,1)} %get-tuple-element.12, bf16[1536,1,768]{2,0,1:T(8,128)(2,1)} %get-tuple-element.6, ...), kind=kLoop, calls=%fused_computation | loop fusion | flops 150994944 | bytes 37748736 | tf_op jit(solution)/shard_map/concatenate | solution.py:78
  123.6 9.6 %fusion.36 = bf16[1,40,2,768]{3,1,2,0:T(8,128)(2,1)S(1)} fusion(bf16[6144,2,768]{2,0,1:T(8,128)(2,1)} %maximum_maximum_fusion, bf16[1,40,6144]{2,1,0:T(8,128)(2,1)} %param.5, f32[40]{0:T(128)S(1)} %copy-done.1), kind=kOutput, calls=%fused_computation.51 | convolution fusion | flops 755097600 | bytes 19488928 | tf_op jit(solution)/shard_map/fjk,kpm->fjpm/dot_general | solution.py:85
  134.1 17.0 %all_to_all.53 = bf16[16,2,1920]{2,1,0:T(2,128)(2,1)} all-to-all(bf16[16,2,1920]{2,1,0:T(2,128)(2,1)S(1)} %reshape.365), channel_id=1, replica_groups=mesh['cons'=16,'blk_0'=2,'blk_1'=8,'blk_2'=2] {'cons'}, dimensions={0} | all-to-all | bytes 245760 | tf_op jit(solution)/shard_map/all_to_all | solution.py:87
  151.1 1.5 reshape.366
  152.6 3.0 convert_bitcast_fusion.1
  155.6 12.0 %copy.26 = bf16[768,2,16,48]{3,2,1,0:T(8,128)(2,1)} copy(bf16[768,2,16,48]{0,2,1,3:T(8,128)(2,1)} %convert_bitcast_fusion.1) | data formatting | bytes 4718592 | tf_op jit(solution)/shard_map/convert_element_type | solution.py:96
  167.6 6.6 %copy.27 = bf16[2,16,768,48]{2,3,1,0:T(8,128)(2,1)} copy(bf16[2,16,768,48]{3,2,0,1:T(8,128)(2,1)} %bitcast.54) | data formatting | bytes 4718592 | tf_op jit(solution)/shard_map/transpose | solution.py:37
  174.2 11.5 %all_to_all.54 = bf16[2,16,768,48]{2,3,1,0:T(8,128)(2,1)} all-to-all(bf16[2,16,768,48]{2,3,1,0:T(8,128)(2,1)} %copy.27), channel_id=1, replica_groups=mesh['cons'=16,'blk_0'=2,'blk_1'=8,'blk_2'=2] {'blk_2'}, dimensions={0} | all-to-all | bytes 4718592 | tf_op jit(solution)/shard_map/all_to_all | solution.py:42
  185.7 3.4 %reduce_sum.24 = bf16[16,768,48]{1,2,0:T(8,128)(2,1)} reduce(bf16[2,16,768,48]{2,3,1,0:T(8,128)(2,1)} %all_to_all.54, bf16[]{:T(256)} %constant.40.clone.1), dimensions={0}, to_apply=%region_0.1 | reduce | flops 589824 | bytes 3538946 | tf_op jit(solution)/shard_map/reduce_sum | solution.py:43
  189.1 41.8 %all_to_all.55 = bf16[16,768,48]{1,2,0:T(8,128)(2,1)} all-to-all(bf16[16,768,48]{1,2,0:T(8,128)(2,1)} %reduce_sum.24), channel_id=1, replica_groups=mesh['cons'=16,'blk_0'=2,'blk_1'=8,'blk_2'=2] {'blk_0','blk_1'}, dimensions={0} | all-to-all | bytes 2359296 | tf_op jit(solution)/shard_map/all_to_all | solution.py:50
  230.9 1.4 reduce_sum.25
  233.5 5.7 %all-to-all-start.3 = ((bf16[16,768,48]{1,2,0:T(8,128)(2,1)}), bf16[16,768,48]{1,2,0:T(8,128)(2,1)}, u32[]{:S(2)}, u32[]{:S(2)}) async-start(bf16[16,768,48]{1,2,0:T(8,128)(2,1)} %broadcast_in_dim.10), calls=%async_computation.3 | async-start | bytes 2359296 | tf_op jit(solution)/shard_map/all_to_all | solution.py:19
  239.2 28.6 %all-to-all-done.3 = bf16[16,768,48]{1,2,0:T(8,128)(2,1)} async-done(((bf16[16,768,48]{1,2,0:T(8,128)(2,1)}), bf16[16,768,48]{1,2,0:T(8,128)(2,1)}, u32[]{:S(2)}, u32[]{:S(2)}) %all-to-all-start.3) | async-done | bytes 1179680 | tf_op jit(solution)/shard_map/all_to_all | solution.py:19
  269.3 8.1 %all_to_all.56 = bf16[2,16,768,48]{2,3,1,0:T(8,128)(2,1)S(1)} all-to-all(bf16[2,16,768,48]{2,3,1,0:T(8,128)(2,1)S(1)} %broadcast_in_dim.11), channel_id=1, replica_groups=mesh['cons'=16,'blk_0'=2,'blk_1'=8,'blk_2'=2] {'blk_2'}, dimensions={0} | all-to-all | bytes 4718592 | tf_op jit(solution)/shard_map/all_to_all | solution.py:19
  277.4 2.7 convert_bitcast_fusion
  280.1 9.2 %copy.28 = f32[16,2,768,48]{3,2,1,0:T(8,128)} copy(f32[16,2,768,48]{2,3,0,1:T(8,128)} %convert_bitcast_fusion) | data formatting | bytes 9437184 | tf_op jit(solution)/shard_map/convert_element_type | solution.py:60
  289.3 8.9 %multiply_convert_fusion = bf16[768,2,16,48]{3,2,1,0:T(8,128)(2,1)} fusion(f32[768,2,16,48]{3,2,1,0:T(8,128)} %bitcast.53, f32[768]{0:T(1024)S(1)} %copy-done.2), kind=kLoop, calls=%fused_computation.1 | loop fusion | flops 2359296 | bytes 7080960 | tf_op jit(solution)/shard_map/convert_element_type | solution.py:101
  298.2 10.0 %copy.29 = bf16[768,2,16,48]{0,2,1,3:T(8,128)(2,1)} copy(bf16[768,2,16,48]{3,2,1,0:T(8,128)(2,1)} %multiply_convert_fusion) | data formatting | bytes 4718592 | tf_op jit(solution)/shard_map/convert_element_type | solution.py:101
  308.2 3.6 %fusion.32 = bf16[16,40,2,48]{1,0,2,3:T(8,128)(2,1)} fusion(bf16[768,2,16,48]{0,2,1,3:T(8,128)(2,1)} %copy.29, bf16[40,48,768,1]{2,1,0,3:T(8,128)(2,1)S(1)} %bitcast.52, f32[48]{0:T(128)S(1)} %compare_select_fusion), kind=kOutput, calls=%fused_computation.48 | convolution fusion | flops 94494720 | bytes 5431488 | tf_op jit(solution)/shard_map/jml,lpgm->gjpm/dot_general | solution.py:104
  313.7 11.3 %all_to_all.57 = bf16[16,2,1920]{2,1,0:T(2,128)(2,1)S(1)} all-to-all(bf16[16,2,1920]{2,1,0:T(2,128)(2,1)S(1)} %reshape.367), channel_id=1, replica_groups=mesh['cons'=16,'blk_0'=2,'blk_1'=8,'blk_2'=2] {'cons'}, dimensions={0} | all-to-all | bytes 245760 | tf_op jit(solution)/shard_map/all_to_all | solution.py:108
  325.7 12.9 %convolution_bitcast_fusion = f32[1,40,6144]{2,1,0:T(8,128)} fusion(bf16[40,2,768]{2,0,1:T(8,128)(2,1)S(1)} %reshape.358, bf16[6144,2,768]{2,0,1:T(8,128)(2,1)} %maximum_maximum_fusion), kind=kOutput, calls=%fused_computation.6 | convolution fusion | flops 754974720 | bytes 19980288 | tf_op jit(solution)/shard_map/fjpm,kpm->fjk/dot_general | solution.py:109
  (22 shorter events, 6.2 us)
Async XLA Ops:
  0.0 152.6 %copy-start = (bf16[40,48,768]{2,1,0:T(8,128)(2,1)S(1)}, bf16[40,48,768]{2,1,0:T(8,128)(2,1)}, u32[]{:S(2)}) copy-start(bf16[40,48,768]{2,1,0:T(8,128)(2,1)} %param.6) | copy-start | bytes 8847364
  102.0 21.5 %copy-start.1 = (f32[40]{0:T(128)S(1)}, f32[40]{0:T(128)}, u32[]{:S(2)}) copy-start(f32[40]{0:T(128)} %param.7) | copy-start | bytes 484
  123.5 29.0 %copy-start.3 = (s32[16]{0:T(128)S(1)}, s32[16]{0:T(128)}, u32[]{:S(2)}) copy-start(s32[16]{0:T(128)} %param.9) | copy-start | bytes 196
  233.5 34.3 %all-to-all-start.3 = ((bf16[16,768,48]{1,2,0:T(8,128)(2,1)}), bf16[16,768,48]{1,2,0:T(8,128)(2,1)}, u32[]{:S(2)}, u32[]{:S(2)}) async-start(bf16[16,768,48]{1,2,0:T(8,128)(2,1)} %broadcast_in_dim.10), calls=%async_computation.3 | async-start | bytes 2359296 | tf_op jit(solution)/shard_map/all_to_all | solution.py:19
  280.1 9.2 %copy-start.2 = (f32[768]{0:T(1024)S(1)}, f32[768]{0:T(1024)}, u32[]{:S(2)}) copy-start(f32[768]{0:T(1024)} %param.8) | copy-start | bytes 9220
where the time goes:
time: 340 us; the launch traced here: 339 us
  other arithmetic  140 us (41%)
  blocking collectives  89.6 us (26%)
  local copies, waits for them, and re-layouts  45.6 us (13%)
  matrix products  29 us (9%)
  waiting for transfers between devices  28.6 us (8%)
  starting transfers between devices  5.71 us (2%)
    convert_element_type x3, other arithmetic, fourier_halves(): cosine = jnp.cos(angles).astype(jnp.bfloat16)  102 us
    all_to_all x1, blocking collectives, summed_rows(): lax.all_to_all(nearer.astype(jnp.bfloat16), far, split_axis=0, concat_axi...  41.8 us
    all_to_all x1, waiting for transfers between devices, from_everyone(): return lax.all_to_all(copies, axis, split_axis=0, concat_axis=0, tiled=True)  28.6 us
    concatenate x1, other arithmetic, local(): jnp.concatenate([fourier_halves(quarter * quarter_len, quarter_len, longi...  21.5 us
    all_to_all x1, blocking collectives, local(): lax.all_to_all(spectra, 'cons', split_axis=3, concat_axis=0, tiled=True)  17 us
    dot_general x1, matrix products, local(): jnp.einsum('fjpm,kpm->fjk', returned, table, preferred_element_type=jnp.f...  12.9 us
    convert_element_type x1, local copies, waits for them, and re-layouts, local(): jnp.einsum('jml,gjpm->lpgm', legendre, ordered, preferred_element_type=jn...  12 us
    all_to_all x1, blocking collectives, sent_and_summed(): lax.all_to_all(in_blocks(array, dim, length), axis, 0, 0, tiled=True)  11.5 us
  transfers between devices with their start and end apart: 1, of which 1 were waited for; matrix products, arithmetic and copies ran while one was open for 0% of the time, Pallas kernels for 0%

commit v1 on v0

v1 whole, which is shorter than its diff:
```python
import math
import numpy as np
import jax
import jax.numpy as jnp
from jax import lax
from jax.experimental import pallas as pl
from jax.experimental.pallas import tpu as pltpu
from jax.sharding import Mesh
from jax.sharding import PartitionSpec as P

RADIX = 48
LANES = 128
CYC = 40
TRI = 3


def by_phase(value, turn):
    re, im = value
    cos, sin = math.cos(2 * math.pi * turn), math.sin(2 * math.pi * turn)
    cos = 0.0 if abs(cos) < 1e-12 else cos
    sin = 0.0 if abs(sin) < 1e-12 else sin

    def scaled(array, factor):
        if array is None or factor == 0.0:
            return None
        if abs(factor - 1.0) < 1e-12:
            return array
        if abs(factor + 1.0) < 1e-12:
            return -array
        return array * np.float32(factor)

    return (
        added(scaled(re, cos), scaled(im, -sin)),
        added(scaled(re, sin), scaled(im, cos)),
    )


def added(a, b):
    if a is None:
        return b
    return a if b is None else a + b


def plus(a, b):
    return added(a[0], b[0]), added(a[1], b[1])


def conj(a):
    return a[0], None if a[1] is None else -a[1]


def at(half, index, length):
    index %= length
    return half[index] if 2 * index <= length else conj(half[length - index])


def factor_of(length):
    return 4 if length % 4 == 0 else (3 if length % 3 == 0 else 2)


def real_fft(values):
    n = len(values)
    if n == 1:
        return [(values[0], None)]
    p = factor_of(n)
    parts = [real_fft(values[i::p]) for i in range(p)]
    out = []
    for k in range(n // 2 + 1):
        total = at(parts[0], k, n // p)
        for i in range(1, p):
            total = plus(total, by_phase(at(parts[i], k, n // p), -i * k / n))
        out.append(total)
    return out


def real_inverse(half, n):
    if n == 1:
        return [half[0][0]]
    p = factor_of(n)
    short = n // p
    out = [None] * n
    for a in range(p):
        folded = []
        for r in range(short // 2 + 1):
            total = (None, None)
            for s in range(p):
                index = r + s * short
                total = plus(total, by_phase(at(half, index, n), index * a / n))
            if r == 0 or 2 * r == short:
                total = (total[0], None)
            folded.append(total)
        for kk, value in enumerate(real_inverse(folded, short)):
            out[p * kk + a] = value
    return out


def phase_tables(period):
    lane = np.arange(LANES)
    turn = np.arange(RADIX)[:, None] * lane[None, :] / period
    twiddle = np.stack([np.cos(2 * np.pi * turn), np.sin(2 * np.pi * turn)], 1)
    q = np.arange(period // RADIX // 8)[:, None] * lane[None, :] / LANES
    cos, sin = np.cos(2 * np.pi * q), np.sin(2 * np.pi * q)
    basis = np.concatenate([np.concatenate([cos, sin], 1), np.concatenate([-sin, cos], 1)], 0)
    return twiddle.reshape(2 * RADIX, LANES).astype(np.float32), basis.astype(jnp.bfloat16)


def forward_kernel(x_ref, weight_ref, twiddle_ref, basis_ref, out_ref, wide, mixed, rows):
    cons = out_ref.shape[0]
    wide[...] = x_ref[...].reshape(wide.shape).astype(jnp.float32)
    for triple in range(RADIX // TRI):
        mixed[triple * LANES + TRI * CYC : (triple + 1) * LANES, :] = jnp.zeros(
            (LANES - TRI * CYC, 2 * LANES), jnp.float32
        )

    @pl.loop(0, CYC // 8)
    def _(group):
        lines = pl.ds(pl.multiple_of(group * 8, 8), 8)
        half = real_fft([wide[lines, k * LANES : (k + 1) * LANES] for k in range(RADIX)])
        for r in range(RADIX):
            re, im = at(half, r, RADIX)
            cos, sin = twiddle_ref[2 * r : 2 * r + 1, :], twiddle_ref[2 * r + 1 : 2 * r + 2, :]
            if im is None:
                new_re, new_im = re * cos, -re * sin
            else:
                new_re, new_im = re * cos + im * sin, im * cos - re * sin
            start = (r // TRI) * LANES + (r % TRI) * CYC
            place = pl.ds(pl.multiple_of(start + group * 8, 8), 8)
            mixed[place, 0:LANES] = new_re
            mixed[place, LANES:] = new_im

    for triple in range(RADIX // TRI):
        block = mixed[triple * LANES : (triple + 1) * LANES, :].astype(jnp.bfloat16)
        got = lax.dot_general(
            basis_ref[...], block, (((1,), (1,)), ((), ())), preferred_element_type=jnp.float32
        )
        rows[triple * 2 * cons : (triple + 1) * 2 * cons, :] = got * weight_ref[...]
    for c in range(cons):
        for h in range(2):
            both = [
                rows[pl.ds(h * 16 * cons + p * cons + c, 8, stride=2 * cons), :] for p in range(2)
            ]
            out_ref[c, h] = jnp.concatenate(both, axis=0).astype(jnp.bfloat16)


def inverse_kernel(z_ref, twiddle_ref, basis_ref, out_ref, rows, mixed):
    cons = z_ref.shape[0]
    for c in range(cons):
        for h in range(2):
            place = (2 * c + h) * 16
            rows[place : place + 16, :] = z_ref[c, h].astype(jnp.float32)
    for triple in range(RADIX // TRI):
        h, t = divmod(triple, 8)
        both = [rows[pl.ds(h * 16 + p * 8 + t, cons, stride=32), :] for p in range(2)]
        lines = jnp.concatenate(both, axis=0).T.astype(jnp.bfloat16)
        mixed[triple * LANES : (triple + 1) * LANES, :] = jnp.dot(
            lines, basis_ref[...], preferred_element_type=jnp.float32
        )

    @pl.loop(0, CYC // 8)
    def _(group):
        turned = []
        for r in range(RADIX):
            start = (r // TRI) * LANES + (r % TRI) * CYC
            place = pl.ds(pl.multiple_of(start + group * 8, 8), 8)
            re, im = mixed[place, 0:LANES], mixed[place, LANES:]
            cos, sin = twiddle_ref[2 * r : 2 * r + 1, :], twiddle_ref[2 * r + 1 : 2 * r + 2, :]
            turned.append((re * cos - im * sin, re * sin + im * cos))
        middle = RADIX // 2
        half = [(turned[0][0], None)]
        for r in range(1, middle):
            pair = plus(turned[r], conj(turned[RADIX - r]))
            half.append((pair[0] * np.float32(0.5), pair[1] * np.float32(0.5)))
        half.append((turned[middle][0], None))
        lines = pl.ds(pl.multiple_of(group * 8, 8), 8)
        for k, value in enumerate(real_inverse(half, RADIX)):
            out_ref[0, lines, k * LANES : (k + 1) * LANES] = value


def forward(elevation, lane_weight, cons):
    period = elevation.shape[-1]
    twiddle, basis = phase_tables(period)
    return pl.pallas_call(
        forward_kernel,
        out_shape=jax.ShapeDtypeStruct((cons, 2, 16, LANES), jnp.bfloat16),
        in_specs=[pl.BlockSpec(memory_space=pltpu.VMEM)] * 4,
        out_specs=pl.BlockSpec(memory_space=pltpu.VMEM),
        scratch_shapes=[
            pltpu.VMEM((CYC, period), jnp.float32),
            pltpu.VMEM((RADIX // TRI * LANES, 2 * LANES), jnp.float32),
            pltpu.VMEM((RADIX // TRI * 2 * cons, LANES), jnp.float32),
        ],
        name="forward",
    )(elevation, lane_weight, jnp.asarray(twiddle), jnp.asarray(basis))


def inverse(pieces, period):
    cons = pieces.shape[0]
    twiddle, basis = phase_tables(period)
    return pl.pallas_call(
        inverse_kernel,
        out_shape=jax.ShapeDtypeStruct((1, CYC, period), jnp.float32),
        in_specs=[pl.BlockSpec(memory_space=pltpu.VMEM)] * 3,
        out_specs=pl.BlockSpec(memory_space=pltpu.VMEM),
        scratch_shapes=[
            pltpu.VMEM((2 * cons * 16, LANES), jnp.float32),
            pltpu.VMEM((RADIX // TRI * LANES, 2 * LANES), jnp.float32),
        ],
        name="inverse",
    )(pieces, jnp.asarray(twiddle), jnp.asarray(basis))


BLK = ("blk_0", "blk_1", "blk_2")


def filled_up(lines, length):
    spare = -lines.shape[0] % length
    if not spare:
        return lines
    return jnp.concatenate([lines, jnp.zeros((spare, *lines.shape[1:]), lines.dtype)])


def from_everyone(array, axis):
    copies = jnp.broadcast_to(array, (lax.axis_size(axis), *array.shape))
    return lax.all_to_all(copies, axis, split_axis=0, concat_axis=0, tiled=True)


def joined_along(tiles, dim):
    dims = list(tiles.shape[1:])
    dims[dim] *= tiles.shape[0]
    return jnp.moveaxis(tiles, 0, dim).reshape(dims)


def gathered_by_axis(array, axes, dim):
    far, near = axes
    tiles = from_everyone(from_everyone(array, far), near)
    return joined_along(tiles.swapaxes(0, 1).reshape(-1, *array.shape), dim)


def in_blocks(array, dim, length):
    dims = array.shape
    tiles = array.reshape(*dims[:dim], length, dims[dim] // length, *dims[dim + 1 :])
    return jnp.moveaxis(tiles, dim, 0)


def sent_and_summed(array, axis, dim):
    length = lax.axis_size(axis)
    tiles = lax.all_to_all(in_blocks(array, dim, length), axis, 0, 0, tiled=True)
    return jnp.sum(tiles.astype(jnp.float32), axis=0)


def summed_rows(array, axes, dim):
    far, near = axes
    tiles = in_blocks(array, dim, lax.axis_size(far))
    nearer = sent_and_summed(tiles, near, dim + 1)
    arrived = lax.all_to_all(
        nearer.astype(jnp.bfloat16), far, split_axis=0, concat_axis=0, tiled=True
    )
    return arrived.astype(jnp.float32).sum(axis=0)


def sum_by_parts(array, axes):
    lines = array.reshape(-1, array.shape[-1])
    padded = filled_up(lines, lax.axis_size(axes[0]) * lax.axis_size(axes[1]))
    whole = gathered_by_axis(summed_rows(padded, axes, 0).astype(jnp.bfloat16), axes, 0)
    return lax.slice_in_dim(whole, 0, len(lines)).reshape(array.shape).astype(jnp.float32)

def local(elevation, legendre, cycle_weight, love_factor, assignment):
    orders_dev = legendre.shape[1]
    cons = lax.axis_size("cons")
    lane_weight = jnp.pad(jnp.tile(cycle_weight, TRI), (0, LANES - TRI * CYC))[None, :]
    pieces = forward(elevation, lane_weight, cons)
    moved = lax.all_to_all(pieces, "cons", split_axis=0, concat_axis=0, tiled=True)
    moved = moved[..., : TRI * CYC].reshape(cons, 2, 2, 8, TRI, CYC)
    one_hot = (assignment[:, None] == jnp.arange(cons, dtype=jnp.int32)[None, :]).astype(
        jnp.bfloat16
    )
    ordered = jnp.einsum(
        "gf,fhptij->ghptij", one_hot, moved, preferred_element_type=jnp.float32
    ).astype(jnp.bfloat16)
    ordered = ordered.transpose(0, 2, 5, 1, 3, 4).reshape(cons, 2, CYC, orders_dev)
    whole = sum_by_parts(
        jnp.einsum("jml,gpjm->mpgl", legendre, ordered, preferred_element_type=jnp.float32).astype(
            jnp.bfloat16
        ),
        (("blk_0", "blk_1"), "blk_2"),
    )
    coefficients = (whole * love_factor).astype(jnp.bfloat16)
    order_index = lax.axis_index("cons") * orders_dev + jnp.arange(orders_dev, dtype=jnp.int32)
    order_factor = jnp.where(order_index == 0, 1.0, 2.0).astype(jnp.float32)
    summed = jnp.einsum(
        "jml,mpgl->gpmj", legendre, coefficients, preferred_element_type=jnp.float32
    )
    synthesis = (summed * order_factor[None, None, :, None]).astype(jnp.bfloat16)
    synthesis = synthesis.reshape(cons, 2, 2, 8, TRI * CYC).transpose(0, 2, 1, 3, 4)
    synthesis = jnp.pad(
        synthesis.reshape(cons, 2, 16, TRI * CYC), ((0, 0),) * 3 + ((0, LANES - TRI * CYC),)
    )
    returned = lax.all_to_all(synthesis, "cons", split_axis=0, concat_axis=0, tiled=True)
    return inverse(returned, elevation.shape[-1])


def solution(mesh):
    torus = Mesh(
        mesh.devices.reshape(mesh.shape["cons"], 2, 8, 2), ("cons", "blk_0", "blk_1", "blk_2")
    )
    placed = (P("cons", BLK, None), P(BLK, "cons", None), P(BLK), P(), P())
    return jax.shard_map(
        local, mesh=torus, in_specs=placed, out_specs=P("cons", BLK, None), check_vma=False
    )
```

time: 340 us -> 146 us (0.43)
  other arithmetic: 140 us -> 5.44 us
  local copies, waits for them, and re-layouts: 45.6 us -> 6.19 us
  matrix products: 29 us -> 3.7 us
  Pallas kernels: 0 us -> 6.96 us
    convert_element_type x4 -> x0, other arithmetic: 111 us -> none  [the longest x3 102 us: fourier_halves(): cosine = jnp.cos(angles).astype(jnp.bfloat16)]
    convert_element_type x5 -> x2, local copies, waits for them, and re-layouts: 33.1 us -> 0.21 us  [the longest x1 0.18 us: local(): (summed * order_factor[None, None, :, None]).astype(jnp.bfloat16)]
    dot_general x4 -> x3, matrix products: 29 us -> 3.7 us  [the longest x1 1.33 us: local(): jnp.einsum('jml,gpjm->mpgl', legendre, ordered, preferred_element_type=jn...]
    concatenate x1 -> x0, other arithmetic: 21.5 us -> none  [local(): jnp.concatenate([fourier_halves(quarter * quarter_len, quarter_len, longi...]
    pallas_call x0 -> x2, Pallas kernels: none -> 6.96 us  [the longest x1 3.67 us: inverse(): pl.pallas_call(inverse_kernel, out_shape=jax.ShapeDtypeStruct((1, CYC, pe...]
    transpose x1 -> x0, local copies, waits for them, and re-layouts: 6.63 us -> none  [in_blocks(): return jnp.moveaxis(tiles, dim, 0)]
where the time goes in v1:
time: 146 us; the launch traced here: 145 us
  blocking collectives  88.2 us (60%)
  waiting for transfers between devices  28.6 us (20%)
  Pallas kernels  6.96 us (5%)
  local copies, waits for them, and re-layouts  6.19 us (4%)
  starting transfers between devices  5.71 us (4%)
  other arithmetic  5.44 us (4%)
  matrix products  3.7 us (3%)
    all_to_all x1, blocking collectives, summed_rows(): lax.all_to_all(nearer.astype(jnp.bfloat16), far, split_axis=0, concat_axi...  41.1 us
    all_to_all x1, waiting for transfers between devices, from_everyone(): return lax.all_to_all(copies, axis, split_axis=0, concat_axis=0, tiled=True)  28.6 us
    all_to_all x1, blocking collectives, local(): lax.all_to_all(pieces, 'cons', split_axis=0, concat_axis=0, tiled=True)  17.2 us
    all_to_all x1, blocking collectives, local(): lax.all_to_all(synthesis, 'cons', split_axis=0, concat_axis=0, tiled=True)  12.1 us
    all_to_all x1, blocking collectives, sent_and_summed(): lax.all_to_all(in_blocks(array, dim, length), axis, 0, 0, tiled=True)  9.66 us
    all_to_all x1, blocking collectives, from_everyone(): return lax.all_to_all(copies, axis, split_axis=0, concat_axis=0, tiled=True)  8.1 us
    all_to_all x1, starting transfers between devices, from_everyone(): return lax.all_to_all(copies, axis, split_axis=0, concat_axis=0, tiled=True)  5.71 us
    pallas_call x1, Pallas kernels, inverse(): pl.pallas_call(inverse_kernel, out_shape=jax.ShapeDtypeStruct((1, CYC, pe...  3.67 us
  transfers between devices with their start and end apart: 1, of which 1 were waited for; matrix products, arithmetic and copies ran while one was open for 0% of the time, Pallas kernels for 0%

profile of v1, /device:TPU:1, one launch (start us, length us, event | category | flops | bytes accessed | tf_op | source)
XLA Modules:
  0.0 144.9 jit_solution(6111435042411252037)
XLA Ops:
  0.0 0.8 tile.4
  0.9 0.6 pad_bitcast_fusion.weight_ref
  1.5 3.3 %forward.1 = bf16[16,2,16,128]{3,2,1,0:T(8,128)(2,1)} custom-call(bf16[1,40,6144]{2,1,0:T(8,128)(2,1)} %x_ref.1, f32[1,128]{1,0:T(1,128)} %pad_bitcast_fusion.weight_ref, f32[96,128]{1,0:T(8,128)} %constant.26.clone.twiddle_ref, bf16[32,256]{1,0:T(8,128)(2,1)} %constant.27.clone.basis_ref), custom_call_target="tpu_custom_call" | custom-call | tf_op jit(solution)/shard_map/forward/pallas_call | solution.py:182
  4.8 17.2 %all_to_all.30 = bf16[16,2,16,128]{3,2,1,0:T(8,128)(2,1)} all-to-all(bf16[16,2,16,128]{3,2,1,0:T(8,128)(2,1)} %forward.1), channel_id=1, replica_groups=mesh['cons'=16,'blk_0'=2,'blk_1'=8,'blk_2'=2] {'cons'}, dimensions={0} | all-to-all | bytes 262144 | tf_op jit(solution)/shard_map/all_to_all | solution.py:272
  22.0 1.4 reshape.23
  23.5 1.1 fusion.14
  24.6 1.3 fusion.5
  25.9 0.2 copy.72
  26.1 9.7 %all_to_all.31 = bf16[2,16,48,768]{3,2,1,0:T(8,128)(2,1)} all-to-all(bf16[2,16,48,768]{3,2,1,0:T(8,128)(2,1)S(1)} %bitcast.36), channel_id=1, replica_groups=mesh['cons'=16,'blk_0'=2,'blk_1'=8,'blk_2'=2] {'blk_2'}, dimensions={0} | all-to-all | bytes 4718592 | tf_op jit(solution)/shard_map/all_to_all | solution.py:247
  35.8 3.4 %reduce_sum.24 = bf16[16,48,768]{2,1,0:T(8,128)(2,1)} reduce(bf16[2,16,48,768]{3,2,1,0:T(8,128)(2,1)} %all_to_all.31, bf16[]{:T(256)} %constant.9.clone.1), dimensions={0}, to_apply=%region_0.1 | reduce | flops 589824 | bytes 3538946 | tf_op jit(solution)/shard_map/reduce_sum | solution.py:248
  39.2 41.1 %all_to_all.32 = bf16[16,48,768]{2,1,0:T(8,128)(2,1)} all-to-all(bf16[16,48,768]{2,1,0:T(8,128)(2,1)} %reduce_sum.24), channel_id=1, replica_groups=mesh['cons'=16,'blk_0'=2,'blk_1'=8,'blk_2'=2] {'blk_0','blk_1'}, dimensions={0} | all-to-all | bytes 2359296 | tf_op jit(solution)/shard_map/all_to_all | solution.py:255
  80.3 1.4 reduce_sum.25
  81.7 1.1 broadcast_in_dim.22
  82.8 5.7 %all-to-all-start.3 = ((bf16[16,48,768]{2,1,0:T(8,128)(2,1)}), bf16[16,48,768]{2,1,0:T(8,128)(2,1)}, u32[]{:S(2)}, u32[]{:S(2)}) async-start(bf16[16,48,768]{2,1,0:T(8,128)(2,1)} %broadcast_in_dim.22), calls=%async_computation.3 | async-start | bytes 2359296 | tf_op jit(solution)/shard_map/all_to_all | solution.py:224
  88.6 28.6 %all-to-all-done.3 = bf16[16,48,768]{2,1,0:T(8,128)(2,1)} async-done(((bf16[16,48,768]{2,1,0:T(8,128)(2,1)}), bf16[16,48,768]{2,1,0:T(8,128)(2,1)}, u32[]{:S(2)}, u32[]{:S(2)}) %all-to-all-start.3) | async-done | bytes 1179680 | tf_op jit(solution)/shard_map/all_to_all | solution.py:224
  117.2 1.4 broadcast_in_dim.23
  118.6 8.1 %all_to_all.33 = bf16[2,16,48,768]{3,2,1,0:T(8,128)(2,1)S(1)} all-to-all(bf16[2,16,48,768]{3,2,1,0:T(8,128)(2,1)S(1)} %broadcast_in_dim.23), channel_id=1, replica_groups=mesh['cons'=16,'blk_0'=2,'blk_1'=8,'blk_2'=2] {'blk_2'}, dimensions={0} | all-to-all | bytes 4718592 | tf_op jit(solution)/shard_map/all_to_all | solution.py:224
  126.7 0.6 copy_convert_fusion
  127.3 0.1 copy-done.1
  127.4 1.3 fusion.15
  128.7 0.2 copy.44
  128.9 0.2 reshape.25
  129.2 12.1 %all_to_all.34.z_ref = bf16[16,2,16,128]{3,2,1,0:T(8,128)(2,1)} all-to-all(bf16[16,2,16,128]{3,2,1,0:T(8,128)(2,1)S(1)} %pad.9), channel_id=1, replica_groups=mesh['cons'=16,'blk_0'=2,'blk_1'=8,'blk_2'=2] {'cons'}, dimensions={0} | all-to-all | bytes 262144 | tf_op jit(solution)/shard_map/all_to_all | solution.py:298
  141.2 3.7 %inverse.1 = f32[1,40,6144]{2,1,0:T(8,128)} custom-call(bf16[16,2,16,128]{3,2,1,0:T(8,128)(2,1)} %all_to_all.34.z_ref, f32[96,128]{1,0:T(8,128)} %constant.26.clone.twiddle_ref, bf16[32,256]{1,0:T(8,128)(2,1)} %constant.27.clone.basis_ref), custom_call_target="tpu_custom_call" | custom-call | tf_op jit(solution)/shard_map/inverse/pallas_call | solution.py:199
  (8 shorter events, 0.2 us)
Async XLA Ops:
  0.0 24.6 %copy-start = (bf16[40,48,768]{2,1,0:T(8,128)(2,1)S(1)}, bf16[40,48,768]{2,1,0:T(8,128)(2,1)}, u32[]{:S(2)}) copy-start(bf16[40,48,768]{2,1,0:T(8,128)(2,1)} %param.10) | copy-start | bytes 8847364
  82.8 34.4 %all-to-all-start.3 = ((bf16[16,48,768]{2,1,0:T(8,128)(2,1)}), bf16[16,48,768]{2,1,0:T(8,128)(2,1)}, u32[]{:S(2)}, u32[]{:S(2)}) async-start(bf16[16,48,768]{2,1,0:T(8,128)(2,1)} %broadcast_in_dim.22), calls=%async_computation.3 | async-start | bytes 2359296 | tf_op jit(solution)/shard_map/all_to_all | solution.py:224
  126.7 0.7 copy-start.1

commit v2 on v1

--- a/solution.py
+++ b/solution.py
@@ -1,3 +1,4 @@
+import functools
 import math
 import numpy as np
 import jax
@@ -5,7 +6,6 @@
 from jax import lax
 from jax.experimental import pallas as pl
 from jax.experimental.pallas import tpu as pltpu
-from jax.sharding import Mesh
 from jax.sharding import PartitionSpec as P
 
 RADIX = 48
@@ -209,101 +209,340 @@
     )(pieces, jnp.asarray(twiddle), jnp.asarray(basis))
 
 
-BLK = ("blk_0", "blk_1", "blk_2")
-
-
-def filled_up(lines, length):
-    spare = -lines.shape[0] % length
-    if not spare:
-        return lines
-    return jnp.concatenate([lines, jnp.zeros((spare, *lines.shape[1:]), lines.dtype)])
-
-
-def from_everyone(array, axis):
-    copies = jnp.broadcast_to(array, (lax.axis_size(axis), *array.shape))
-    return lax.all_to_all(copies, axis, split_axis=0, concat_axis=0, tiled=True)
-
-
-def joined_along(tiles, dim):
-    dims = list(tiles.shape[1:])
-    dims[dim] *= tiles.shape[0]
-    return jnp.moveaxis(tiles, 0, dim).reshape(dims)
-
-
-def gathered_by_axis(array, axes, dim):
-    far, near = axes
-    tiles = from_everyone(from_everyone(array, far), near)
-    return joined_along(tiles.swapaxes(0, 1).reshape(-1, *array.shape), dim)
-
-
-def in_blocks(array, dim, length):
-    dims = array.shape
-    tiles = array.reshape(*dims[:dim], length, dims[dim] // length, *dims[dim + 1 :])
-    return jnp.moveaxis(tiles, dim, 0)
-
-
-def sent_and_summed(array, axis, dim):
-    length = lax.axis_size(axis)
-    tiles = lax.all_to_all(in_blocks(array, dim, length), axis, 0, 0, tiled=True)
-    return jnp.sum(tiles.astype(jnp.float32), axis=0)
-
-
-def summed_rows(array, axes, dim):
-    far, near = axes
-    tiles = in_blocks(array, dim, lax.axis_size(far))
-    nearer = sent_and_summed(tiles, near, dim + 1)
-    arrived = lax.all_to_all(
-        nearer.astype(jnp.bfloat16), far, split_axis=0, concat_axis=0, tiled=True
-    )
-    return arrived.astype(jnp.float32).sum(axis=0)
-
-
-def sum_by_parts(array, axes):
-    lines = array.reshape(-1, array.shape[-1])
-    padded = filled_up(lines, lax.axis_size(axes[0]) * lax.axis_size(axes[1]))
-    whole = gathered_by_axis(summed_rows(padded, axes, 0).astype(jnp.bfloat16), axes, 0)
-    return lax.slice_in_dim(whole, 0, len(lines)).reshape(array.shape).astype(jnp.float32)
+MESH = pl.DeviceIdType.MESH
+F32 = jnp.float32
+BF16 = jnp.bfloat16
+KERNEL_ID = 0
+
+
+def middle_kernel(
+    ring, cons, pieces, legendre, love, assignment, out,
+    held, wide, table, got, mixed, lines, part, first, later, staged, sent, other, coef,
+    rows, back, returned,
+    own_sem, swap_send, swap_recv, out_send, out_recv, sum_send, sum_recv, pair_send, pair_recv,
+    all_send, all_recv, back_send, back_recv,
+):
+    c, b = lax.axis_index("cons"), lax.axis_index("blk")
+    core = lax.rem(b, 2)
+    z = lax.rem(b // 2, ring)
+    line = b // (2 * ring)
+    chip = b - core
+    me = 2 * c + core
+    peers = 2 * cons
+    far = ring // 2
+    depth = legendre.shape[2]
+    half_orders = TRI * ring
+    full = 2 * cons
+    barrier = pltpu.get_barrier_semaphore()
+
+    def slot(offset):
+        return lax.rem(z + offset + ring, ring)
+
+    def on_ring(offset):
+        return (c, line * 2 * ring + slot(offset) * 2 + core)
+
+    def peer(offset):
+        index = lax.rem(me + offset, peers)
+        return index // 2, lax.rem(index, 2)
+
+    def remote(source, target, send, recv, device):
+        return pltpu.make_async_remote_copy(
+            src_ref=source,
+            dst_ref=target,
+            send_sem=send,
+            recv_sem=recv,
+            device_id=device,
+            device_id_type=MESH,
+        )
+
+    def exchange(offset, source, landing, send, recv):
+        there = peer(offset)
+        return remote(
+            source.at[there[0], there[1]],
+            landing.at[c, core],
+            send.at[offset],
+            recv.at[offset],
+            (there[0], chip + there[1]),
+        )
+
+    across = (c, (1 - line) * 2 * ring + z * 2 + core)
+
+    @pl.loop(1, peers)
+    def _(offset):
+        there = peer(offset)
+        pl.semaphore_signal(
+            barrier, inc=1, device_id=(there[0], chip + there[1]), device_id_type=MESH
+        )
+
+    for target in (on_ring(1), on_ring(-1), across):
+        pl.semaphore_signal(barrier, inc=1, device_id=target, device_id_type=MESH)
+
+    def half_of(which):
+        return legendre.at[:, pl.ds(pl.multiple_of(which * half_orders, 8), half_orders), :]
+
+    mine = pltpu.make_async_copy(half_of(core), held.at[core], own_sem)
+    mine.start()
+    pl.semaphore_wait(barrier, peers + 2)
+
+    swap = remote(half_of(1 - core), held.at[core], swap_send, swap_recv, (c, chip + 1 - core))
+    swap.start()
+
+    @pl.loop(1, peers)
+    def _(offset):
+        exchange(offset, pieces, got, out_send, out_recv).start()
+
+    got[c, core] = pieces[c, core]
+
+    def turn(which):
+        @pl.loop(0, CYC)
+        def _(j):
+            place = pl.ds(pl.multiple_of(j * half_orders, 8), half_orders)
+            for tile in range(depth // LANES):
+                wide[tile, place, :] = held[
+                    which, j, :, tile * LANES : (tile + 1) * LANES
+                ].astype(F32)
+
+        @pl.loop(0, ring)
+        def _(t):
+            place = pl.ds(pl.multiple_of(which * LANES, LANES), LANES)
+            for tile in range(depth // LANES):
+                taken = [
+                    wide[tile, pl.ds(TRI * t + i, CYC, stride=half_orders), :] for i in range(TRI)
+                ]
+                taken.append(jnp.zeros((LANES - TRI * CYC, LANES), F32))
+                table[t, place, tile * LANES : (tile + 1) * LANES] = jnp.concatenate(
+                    taken, axis=0
+                ).astype(BF16)
+
+    mine.wait()
+    turn(core)
+    swap.wait()
+    turn(1 - core)
+
+    @pl.loop(1, peers)
+    def _(offset):
+        exchange(offset, pieces, got, out_send, out_recv).wait()
+
+    for g in range(cons):
+        field = assignment[g]
+        for s in range(2):
+            mixed[(s * cons + g) * 16 : (s * cons + g + 1) * 16, :] = got[field, s].astype(F32)
+    for t in range(ring):
+        for s in range(2):
+            for p in range(2):
+                lines[t, p * cons : (p + 1) * cons, s * LANES : (s + 1) * LANES] = mixed[
+                    pl.ds(s * cons * 16 + p * 8 + t, cons, stride=16), :
+                ]
+
+    lane = lax.broadcasted_iota(jnp.int32, (full, 2 * LANES), 1)
+    lane = jnp.where(lane >= LANES, lane - LANES, lane)
+    which = jnp.where(lane < CYC, 0, jnp.where(lane < 2 * CYC, 1, jnp.where(lane < TRI * CYC, 2, 3)))
+
+    def analysed(t):
+        x = lines[t]
+        left = [jnp.where(which == i, x, 0.0) for i in range(TRI)]
+        part[t] = jnp.dot(
+            jnp.concatenate(left, axis=0).astype(BF16), table[t], preferred_element_type=F32
+        ).astype(BF16)
+
+    def block(i):
+        return pl.ds(i * full, full)
+
+    def piece(i, p):
+        return pl.ds(i * full + p * cons, cons)
+
+    ways = (1, -1)
+
+    def sum_step(way, step, i):
+        device = on_ring(ways[way])
+        send, recv = sum_send.at[way, step, i], sum_recv.at[way, step, i]
+        if step == 0:
+            return remote(part.at[slot(far), piece(i, way)], first.at[way, i], send, recv, device)
+        return remote(staged.at[way, step - 1, i], later.at[way, step - 1, i], send, recv, device)
+
+    analysed(slot(far))
+    for i in range(TRI):
+        for way in range(2):
+            sum_step(way, 0, i).start()
+    for step in range(1, far):
+        for way in range(2):
+            analysed(slot(ways[way] * (far - step)))
+        for i in range(TRI):
+            for way in range(2):
+                owner = slot(ways[way] * (far - step))
+                sum_step(way, step - 1, i).wait_recv()
+                if step == 1:
+                    for p in range(2):
+                        value = part[owner, piece(i, p), :]
+                        if p == way:
+                            value = (value.astype(F32) + first[way, i].astype(F32)).astype(BF16)
+                        staged[way, 0, i, p * cons : (p + 1) * cons, :] = value
+                else:
+                    staged[way, step - 1, i] = (
+                        part[owner, block(i), :].astype(F32) + later[way, step - 2, i].astype(F32)
+                    ).astype(BF16)
+                sum_step(way, step, i).start()
+    analysed(z)
+
+    def pair_step(i):
+        return remote(sent.at[i], other.at[i], pair_send.at[i], pair_recv.at[i], across)
+
+    for i in range(TRI):
+        for way in range(2):
+            sum_step(way, far - 1, i).wait_recv()
+        sent[i] = (
+            part[z, block(i), :].astype(F32)
+            + later[0, far - 2, i].astype(F32)
+            + later[1, far - 2, i].astype(F32)
+        ).astype(BF16)
+        pair_step(i).start()
+
+    def all_step(way, step, i):
+        place = piece(i, way) if step == far - 1 else block(i)
+        ref = coef.at[slot(-ways[way] * step), place]
+        return remote(
+            ref, ref, all_send.at[way, step, i], all_recv.at[way, step, i], on_ring(ways[way])
+        )
+
+    def all_arrival(way, step, i):
+        place = piece(i, way) if step == far - 1 else block(i)
+        ref = coef.at[slot(-ways[way] * (step + 1)), place]
+        return remote(
+            ref, ref, all_send.at[way, step, i], all_recv.at[way, step, i], on_ring(ways[way])
+        )
+
+    scale = love[...]
+    for i in range(TRI):
+        pair_step(i).wait_recv()
+        coef[z, block(i), :] = (
+            (sent[i].astype(F32) + other[i].astype(F32)) * scale
+        ).astype(BF16)
+        for way in range(2):
+            all_step(way, 0, i).start()
+
+    def synthesised(t):
+        got_all = lax.dot_general(
+            coef[t], table[t], (((1,), (1,)), ((), ())), preferred_element_type=F32
+        )
+        chosen = jnp.where(
+            which == 0, got_all[:full], jnp.where(which == 1, got_all[full : 2 * full], got_all[2 * full :])
+        )
+        order = which + (TRI * t + core * half_orders + c * 2 * half_orders)
+        chosen = chosen * jnp.where(order == 0, 1.0, 2.0).astype(F32)
+        for s in range(2):
+            place = pl.ds(pl.multiple_of(s * ring * full + t * full, 8), full)
+            rows[place, :] = chosen[:, s * LANES : (s + 1) * LANES]
+
+    for step in range(1, far):
+        for i in range(TRI):
+            for way in range(2):
+                all_arrival(way, step - 1, i).wait_recv()
+                all_step(way, step, i).start()
+        if step == 1:
+            synthesised(z)
+        else:
+            for way in ways:
+                synthesised(slot(-way * (step - 1)))
+    for way in ways:
+        synthesised(slot(-way * (far - 1)))
+    for i in range(TRI):
+        for way in range(2):
+            all_arrival(way, far - 1, i).wait_recv()
+    synthesised(slot(far))
+
+    for g in range(cons):
+        for s in range(2):
+            both = [
+                rows[pl.ds(s * ring * full + p * cons + g, ring, stride=full), :] for p in range(2)
+            ]
+            back[g, s] = jnp.concatenate(both, axis=0).astype(BF16)
+
+    @pl.loop(1, peers)
+    def _(offset):
+        exchange(offset, back, returned, back_send, back_recv).start()
+
+    returned[c, core] = back[c, core]
+
+    for i in range(TRI):
+        pair_step(i).wait_send()
+        for way in range(2):
+            for step in range(far):
+                sum_step(way, step, i).wait_send()
+                all_step(way, step, i).wait_send()
+
+    @pl.loop(1, peers)
+    def _(offset):
+        exchange(offset, back, returned, back_send, back_recv).wait()
+
+    out[...] = returned[...]
+
+
+def middle(pieces, legendre, love, assignment):
+    cons = pieces.shape[0]
+    depth = legendre.shape[2]
+    ring = 8
+    far = ring // 2
+    full = 2 * cons
+    dma = pltpu.SemaphoreType.DMA
+    vmem = pltpu.VMEM
+    return pl.pallas_call(
+        functools.partial(middle_kernel, ring, cons),
+        out_shape=jax.ShapeDtypeStruct(pieces.shape, BF16),
+        in_specs=[
+            pl.BlockSpec(memory_space=pltpu.VMEM),
+            pl.BlockSpec(memory_space=pl.ANY),
+            pl.BlockSpec(memory_space=pltpu.VMEM),
+            pl.BlockSpec(memory_space=pltpu.SMEM),
+        ],
+        out_specs=pl.BlockSpec(memory_space=pltpu.VMEM),
+        scratch_shapes=[
+            vmem((2, CYC, TRI * ring, depth), BF16),
+            vmem((depth // LANES, CYC * TRI * ring, LANES), F32),
+            vmem((ring, 2 * LANES, depth), BF16),
+            vmem(pieces.shape, BF16),
+            vmem((2 * cons * 16, LANES), F32),
+            vmem((ring, full, 2 * LANES), F32),
+            vmem((ring, TRI * full, depth), BF16),
+            vmem((2, TRI, cons, depth), BF16),
+            vmem((2, far - 1, TRI, full, depth), BF16),
+            vmem((2, far - 1, TRI, full, depth), BF16),
+            vmem((TRI, full, depth), BF16),
+            vmem((TRI, full, depth), BF16),
+            vmem((ring, TRI * full, depth), BF16),
+            vmem((2 * ring * full, LANES), F32),
+            vmem(pieces.shape, BF16),
+            vmem(pieces.shape, BF16),
+            dma,
+            dma,
+            dma,
+            dma((2 * cons,)),
+            dma((2 * cons,)),
+            dma((2, far, TRI)),
+            dma((2, far, TRI)),
+            dma((TRI,)),
+            dma((TRI,)),
+            dma((2, far, TRI)),
+            dma((2, far, TRI)),
+            dma((2 * cons,)),
+            dma((2 * cons,)),
+        ],
+        compiler_params=pltpu.CompilerParams(
+            collective_id=KERNEL_ID, has_side_effects=True, vmem_limit_bytes=50 * 2**20
+        ),
+        name="middle",
+    )(pieces, legendre, love, assignment)
+
 
 def local(elevation, legendre, cycle_weight, love_factor, assignment):
-    orders_dev = legendre.shape[1]
     cons = lax.axis_size("cons")
     lane_weight = jnp.pad(jnp.tile(cycle_weight, TRI), (0, LANES - TRI * CYC))[None, :]
     pieces = forward(elevation, lane_weight, cons)
-    moved = lax.all_to_all(pieces, "cons", split_axis=0, concat_axis=0, tiled=True)
-    moved = moved[..., : TRI * CYC].reshape(cons, 2, 2, 8, TRI, CYC)
-    one_hot = (assignment[:, None] == jnp.arange(cons, dtype=jnp.int32)[None, :]).astype(
-        jnp.bfloat16
+    returned = middle(pieces, legendre, love_factor[None, :], assignment)
+    return inverse(returned, elevation.shape[-1])
+
+
+def solution(mesh):
+    placed = (P("cons", "blk", None), P("blk", "cons", None), P("blk"), P(), P())
+    return jax.shard_map(
+        local, mesh=mesh, in_specs=placed, out_specs=P("cons", "blk", None), check_vma=False
     )
-    ordered = jnp.einsum(
-        "gf,fhptij->ghptij", one_hot, moved, preferred_element_type=jnp.float32
-    ).astype(jnp.bfloat16)
-    ordered = ordered.transpose(0, 2, 5, 1, 3, 4).reshape(cons, 2, CYC, orders_dev)
-    whole = sum_by_parts(
-        jnp.einsum("jml,gpjm->mpgl", legendre, ordered, preferred_element_type=jnp.float32).astype(
-            jnp.bfloat16
-        ),
-        (("blk_0", "blk_1"), "blk_2"),
-    )
-    coefficients = (whole * love_factor).astype(jnp.bfloat16)
-    order_index = lax.axis_index("cons") * orders_dev + jnp.arange(orders_dev, dtype=jnp.int32)
-    order_factor = jnp.where(order_index == 0, 1.0, 2.0).astype(jnp.float32)
-    summed = jnp.einsum(
-        "jml,mpgl->gpmj", legendre, coefficients, preferred_element_type=jnp.float32
-    )
-    synthesis = (summed * order_factor[None, None, :, None]).astype(jnp.bfloat16)
-    synthesis = synthesis.reshape(cons, 2, 2, 8, TRI * CYC).transpose(0, 2, 1, 3, 4)
-    synthesis = jnp.pad(
-        synthesis.reshape(cons, 2, 16, TRI * CYC), ((0, 0),) * 3 + ((0, LANES - TRI * CYC),)
-    )
-    returned = lax.all_to_all(synthesis, "cons", split_axis=0, concat_axis=0, tiled=True)
-    return inverse(returned, elevation.shape[-1])
-
-
-def solution(mesh):
-    torus = Mesh(
-        mesh.devices.reshape(mesh.shape["cons"], 2, 8, 2), ("cons", "blk_0", "blk_1", "blk_2")
-    )
-    placed = (P("cons", BLK, None), P(BLK, "cons", None), P(BLK), P(), P())
-    return jax.shard_map(
-        local, mesh=torus, in_specs=placed, out_specs=P("cons", BLK, None), check_vma=False
-    )

time: 146 us -> 79.7 us (0.55)
  blocking collectives: 88.2 us -> 0 us
  Pallas kernels: 6.96 us -> 73.4 us
  waiting for transfers between devices: 28.6 us -> 0 us
  starting transfers between devices: 5.71 us -> 0 us
  other arithmetic: 5.44 us -> 0 us
  matrix products: 3.7 us -> 0 us
    all_to_all x5 -> x0, blocking collectives: 88.2 us -> none  [the longest x1 41.1 us: summed_rows(): lax.all_to_all(nearer.astype(jnp.bfloat16), far, split_axis=0, concat_axi...]
    pallas_call x0 -> x1, Pallas kernels: none -> 66.5 us  [middle(): pl.pallas_call(functools.partial(middle_kernel, ring, cons), out_shape=ja...]
    all_to_all x1 -> x0, waiting for transfers between devices: 28.6 us -> none  [from_everyone(): return lax.all_to_all(copies, axis, split_axis=0, concat_axis=0, tiled=True)]
    all_to_all x1 -> x0, starting transfers between devices: 5.71 us -> none  [from_everyone(): return lax.all_to_all(copies, axis, split_axis=0, concat_axis=0, tiled=True)]
    reduce_sum x2 -> x0, other arithmetic: 4.86 us -> none  [the longest x1 3.42 us: sent_and_summed(): return jnp.sum(tiles.astype(jnp.float32), axis=0)]
    unnamed x4 -> x8, local copies, waits for them, and re-layouts: 0.11 us -> 4.03 us
    dot_general x3 -> x0, matrix products: 3.7 us -> none  [the longest x1 1.33 us: local(): jnp.einsum('jml,gpjm->mpgl', legendre, ordered, preferred_element_type=jn...]
    broadcast_in_dim x2 -> x1, local copies, waits for them, and re-layouts: 2.55 us -> 0.69 us  [local(): returned = middle(pieces, legendre, love_factor[None, :], assignment)]
  transfers between devices with their start and end apart: 1 -> 0, of which waited for: 1 -> 0; matrix products, arithmetic and copies ran while one was open for 0% -> 0% of each run, Pallas kernels for 0% -> 0%
where the time goes in v2:
time: 79.7 us; the launch traced here: 79.5 us
  Pallas kernels  73.4 us (92%)
  local copies, waits for them, and re-layouts  6 us (8%)
    pallas_call x1, Pallas kernels, middle(): pl.pallas_call(functools.partial(middle_kernel, ring, cons), out_shape=ja...  66.5 us
    unnamed x8, local copies, waits for them, and re-layouts  4.03 us
    pallas_call x1, Pallas kernels, inverse(): pl.pallas_call(inverse_kernel, out_shape=jax.ShapeDtypeStruct((1, CYC, pe...  3.66 us
    pallas_call x1, Pallas kernels, forward(): pl.pallas_call(forward_kernel, out_shape=jax.ShapeDtypeStruct((cons, 2, 1...  3.29 us

profile of v2, /device:TPU:1, one launch (start us, length us, event | category | flops | bytes accessed | tf_op | source)
XLA Modules:
  0.0 79.5 jit_solution(2876930855894053581)
XLA Ops:
  0.0 0.7 tile.4
  0.7 0.1 tile.10
  0.7 0.5 pad_bitcast_fusion.weight_ref
  1.3 0.7 broadcast_in_dim.7.love
  2.0 3.3 %forward.1.pieces = bf16[16,2,16,128]{3,2,1,0:T(8,128)(2,1)} custom-call(bf16[1,40,6144]{2,1,0:T(8,128)(2,1)} %x_ref.1, f32[1,128]{1,0:T(1,128)} %pad_bitcast_fusion.weight_ref, f32[96,128]{1,0:T(8,128)} %constant.7.clone.twiddle_ref, bf16[32,256]{1,0:T(8,128)(2,1)} %constant.8.clone.basis_ref), custom_call_target="tpu_custom_call" | custom-call | tf_op jit(solution)/shard_map/forward/pallas_call | solution.py:182
  5.3 0.0 copy-start
  5.3 1.8 %copy-done = bf16[40,48,768]{2,1,0:T(8,128)(2,1)S(1)} copy-done((bf16[40,48,768]{2,1,0:T(8,128)(2,1)S(1)}, bf16[40,48,768]{2,1,0:T(8,128)(2,1)}, u32[]{:S(2)}) %copy-start) | copy-done | bytes 2949144
  7.1 0.0 copy-start.2
  7.1 0.9 %copy-done.2 = bf16[16,2,16,128]{3,2,1,0:T(8,128)(2,1)S(1)} copy-done((bf16[16,2,16,128]{3,2,1,0:T(8,128)(2,1)S(1)}, bf16[16,2,16,128]{3,2,1,0:T(8,128)(2,1)}, u32[]{:S(2)}) %copy-start.2) | copy-done | bytes 131096
  8.0 0.0 copy-start.3
  8.0 0.7 copy-done.3
  8.7 66.5 %middle.1.z_ref = bf16[16,2,16,128]{3,2,1,0:T(8,128)(2,1)S(1)} custom-call(bf16[16,2,16,128]{3,2,1,0:T(8,128)(2,1)S(1)} %copy-done.2, bf16[40,48,768]{2,1,0:T(8,128)(2,1)S(1)} %copy-done, f32[1,768]{1,0:T(1,128)S(1)} %broadcast_in_dim.7.love, s32[16]{0:T(128)S(1)} %copy-done.3), custom_call_target="tpu_custom_call" | custom-call | tf_op jit(solution)/shard_map/middle/pallas_call | solution.py:488
  75.1 0.0 copy-start.1
  75.2 0.6 copy-done.1
  75.8 3.7 %inverse.1 = f32[1,40,6144]{2,1,0:T(8,128)} custom-call(bf16[16,2,16,128]{3,2,1,0:T(8,128)(2,1)} %copy-done.1, f32[96,128]{1,0:T(8,128)} %constant.7.clone.twiddle_ref, bf16[32,256]{1,0:T(8,128)(2,1)} %constant.8.clone.basis_ref), custom_call_target="tpu_custom_call" | custom-call | tf_op jit(solution)/shard_map/inverse/pallas_call | solution.py:199
Async XLA Ops:
  5.3 1.8 %copy-start = (bf16[40,48,768]{2,1,0:T(8,128)(2,1)S(1)}, bf16[40,48,768]{2,1,0:T(8,128)(2,1)}, u32[]{:S(2)}) copy-start(bf16[40,48,768]{2,1,0:T(8,128)(2,1)} %legendre.1) | copy-start | bytes 8847364
  7.1 0.9 %copy-start.2 = (bf16[16,2,16,128]{3,2,1,0:T(8,128)(2,1)S(1)}, bf16[16,2,16,128]{3,2,1,0:T(8,128)(2,1)}, u32[]{:S(2)}) copy-start(bf16[16,2,16,128]{3,2,1,0:T(8,128)(2,1)} %forward.1.pieces) | copy-start | bytes 393220
  8.0 0.7 copy-start.3
  75.1 0.6 copy-start.1

commit v3 on v2

--- a/solution.py
+++ b/solution.py
@@ -104,13 +104,13 @@
     return twiddle.reshape(2 * RADIX, LANES).astype(np.float32), basis.astype(jnp.bfloat16)
 
 
-def forward_kernel(x_ref, weight_ref, twiddle_ref, basis_ref, out_ref, wide, mixed, rows):
+def transformed(x_ref, weight, twiddle_ref, basis_ref, out_ref, wide, mixed, rows):
     cons = out_ref.shape[0]
-    wide[...] = x_ref[...].reshape(wide.shape).astype(jnp.float32)
     for triple in range(RADIX // TRI):
         mixed[triple * LANES + TRI * CYC : (triple + 1) * LANES, :] = jnp.zeros(
             (LANES - TRI * CYC, 2 * LANES), jnp.float32
         )
+    wide[...] = x_ref[...].reshape(wide.shape).astype(jnp.float32)
 
     @pl.loop(0, CYC // 8)
     def _(group):
@@ -133,7 +133,7 @@
         got = lax.dot_general(
             basis_ref[...], block, (((1,), (1,)), ((), ())), preferred_element_type=jnp.float32
         )
-        rows[triple * 2 * cons : (triple + 1) * 2 * cons, :] = got * weight_ref[...]
+        rows[triple * 2 * cons : (triple + 1) * 2 * cons, :] = got * weight
     for c in range(cons):
         for h in range(2):
             both = [
@@ -176,23 +176,6 @@
             out_ref[0, lines, k * LANES : (k + 1) * LANES] = value
 
 
-def forward(elevation, lane_weight, cons):
-    period = elevation.shape[-1]
-    twiddle, basis = phase_tables(period)
-    return pl.pallas_call(
-        forward_kernel,
-        out_shape=jax.ShapeDtypeStruct((cons, 2, 16, LANES), jnp.bfloat16),
-        in_specs=[pl.BlockSpec(memory_space=pltpu.VMEM)] * 4,
-        out_specs=pl.BlockSpec(memory_space=pltpu.VMEM),
-        scratch_shapes=[
-            pltpu.VMEM((CYC, period), jnp.float32),
-            pltpu.VMEM((RADIX // TRI * LANES, 2 * LANES), jnp.float32),
-            pltpu.VMEM((RADIX // TRI * 2 * cons, LANES), jnp.float32),
-        ],
-        name="forward",
-    )(elevation, lane_weight, jnp.asarray(twiddle), jnp.asarray(basis))
-
-
 def inverse(pieces, period):
     cons = pieces.shape[0]
     twiddle, basis = phase_tables(period)
@@ -205,6 +188,7 @@
             pltpu.VMEM((2 * cons * 16, LANES), jnp.float32),
             pltpu.VMEM((RADIX // TRI * LANES, 2 * LANES), jnp.float32),
         ],
+        compiler_params=pltpu.CompilerParams(vmem_limit_bytes=10 * 2**20),
         name="inverse",
     )(pieces, jnp.asarray(twiddle), jnp.asarray(basis))
 
@@ -216,10 +200,11 @@
 
 
 def middle_kernel(
-    ring, cons, pieces, legendre, love, assignment, out,
+    ring, cons, elevation, legendre, cycle_weight, love_factor, assigned, twiddles, bases, out,
+    height, weights, love, assignment, twiddle, basis, pieces, tall, spun, spread,
     held, wide, table, got, mixed, lines, part, first, later, staged, sent, other, coef,
     rows, back, returned,
-    own_sem, swap_send, swap_recv, out_send, out_recv, sum_send, sum_recv, pair_send, pair_recv,
+    load_sem, own_sem, swap_send, swap_recv, out_send, out_recv, sum_send, sum_recv, pair_send, pair_recv,
     all_send, all_recv, back_send, back_recv,
 ):
     c, b = lax.axis_index("cons"), lax.axis_index("blk")
@@ -282,7 +267,33 @@
 
     mine = pltpu.make_async_copy(half_of(core), held.at[core], own_sem)
     mine.start()
-    pl.semaphore_wait(barrier, peers + 2)
+    pairs = (
+        (elevation, height),
+        (twiddles, twiddle),
+        (bases, basis),
+        (cycle_weight, weights),
+        (assigned, assignment),
+        (love_factor, love),
+    )
+    loads = [
+        pltpu.make_async_copy(source, target, load_sem.at[i])
+        for i, (source, target) in enumerate(pairs)
+    ]
+    for load in loads:
+        load.start()
+    for load in loads:
+        load.wait()
+
+    with jax.named_scope("fft"):
+        lane_of = lax.broadcasted_iota(jnp.int32, (1, LANES), 1)
+        day = lane_of - jnp.where(lane_of < CYC, 0, jnp.where(lane_of < 2 * CYC, CYC, 2 * CYC))
+        weight = jnp.zeros((1, LANES), F32)
+        for j in range(CYC):
+            weight = jnp.where(day == j, weights[j], weight)
+        transformed(height, weight, twiddle, basis, pieces, tall, spun, spread)
+
+    with jax.named_scope("barrier"):
+        pl.semaphore_wait(barrier, peers + 2)
 
     swap = remote(half_of(1 - core), held.at[core], swap_send, swap_recv, (c, chip + 1 - core))
     swap.start()
@@ -314,25 +325,31 @@
                     taken, axis=0
                 ).astype(BF16)
 
-    mine.wait()
-    turn(core)
-    swap.wait()
-    turn(1 - core)
-
-    @pl.loop(1, peers)
-    def _(offset):
-        exchange(offset, pieces, got, out_send, out_recv).wait()
-
-    for g in range(cons):
-        field = assignment[g]
-        for s in range(2):
-            mixed[(s * cons + g) * 16 : (s * cons + g + 1) * 16, :] = got[field, s].astype(F32)
-    for t in range(ring):
-        for s in range(2):
-            for p in range(2):
-                lines[t, p * cons : (p + 1) * cons, s * LANES : (s + 1) * LANES] = mixed[
-                    pl.ds(s * cons * 16 + p * 8 + t, cons, stride=16), :
-                ]
+    with jax.named_scope("turn_own"):
+        mine.wait()
+        turn(core)
+    with jax.named_scope("swap_wait"):
+        swap.wait()
+    with jax.named_scope("turn_other"):
+        turn(1 - core)
+
+    with jax.named_scope("wait_out"):
+
+        @pl.loop(1, peers)
+        def _(offset):
+            exchange(offset, pieces, got, out_send, out_recv).wait()
+
+    with jax.named_scope("lines"):
+        for g in range(cons):
+            field = assignment[g]
+            for s in range(2):
+                mixed[(s * cons + g) * 16 : (s * cons + g + 1) * 16, :] = got[field, s].astype(F32)
+        for t in range(ring):
+            for s in range(2):
+                for p in range(2):
+                    lines[t, p * cons : (p + 1) * cons, s * LANES : (s + 1) * LANES] = mixed[
+                        pl.ds(s * cons * 16 + p * 8 + t, cons, stride=16), :
+                    ]
 
     lane = lax.broadcasted_iota(jnp.int32, (full, 2 * LANES), 1)
     lane = jnp.where(lane >= LANES, lane - LANES, lane)
@@ -360,13 +377,16 @@
             return remote(part.at[slot(far), piece(i, way)], first.at[way, i], send, recv, device)
         return remote(staged.at[way, step - 1, i], later.at[way, step - 1, i], send, recv, device)
 
-    analysed(slot(far))
-    for i in range(TRI):
-        for way in range(2):
-            sum_step(way, 0, i).start()
+    with jax.named_scope("first_part"):
+        analysed(slot(far))
+        for i in range(TRI):
+            for way in range(2):
+                sum_step(way, 0, i).start()
     for step in range(1, far):
+      with jax.named_scope(f"part#s={step}"):
         for way in range(2):
             analysed(slot(ways[way] * (far - step)))
+      with jax.named_scope(f"sum#s={step}"):
         for i in range(TRI):
             for way in range(2):
                 owner = slot(ways[way] * (far - step))
@@ -387,15 +407,16 @@
     def pair_step(i):
         return remote(sent.at[i], other.at[i], pair_send.at[i], pair_recv.at[i], across)
 
-    for i in range(TRI):
-        for way in range(2):
-            sum_step(way, far - 1, i).wait_recv()
-        sent[i] = (
-            part[z, block(i), :].astype(F32)
-            + later[0, far - 2, i].astype(F32)
-            + later[1, far - 2, i].astype(F32)
-        ).astype(BF16)
-        pair_step(i).start()
+    with jax.named_scope("last_sum"):
+        for i in range(TRI):
+            for way in range(2):
+                sum_step(way, far - 1, i).wait_recv()
+            sent[i] = (
+                part[z, block(i), :].astype(F32)
+                + later[0, far - 2, i].astype(F32)
+                + later[1, far - 2, i].astype(F32)
+            ).astype(BF16)
+            pair_step(i).start()
 
     def all_step(way, step, i):
         place = piece(i, way) if step == far - 1 else block(i)
@@ -411,14 +432,15 @@
             ref, ref, all_send.at[way, step, i], all_recv.at[way, step, i], on_ring(ways[way])
         )
 
-    scale = love[...]
-    for i in range(TRI):
-        pair_step(i).wait_recv()
-        coef[z, block(i), :] = (
-            (sent[i].astype(F32) + other[i].astype(F32)) * scale
-        ).astype(BF16)
-        for way in range(2):
-            all_step(way, 0, i).start()
+    scale = love[...].reshape(1, depth)
+    with jax.named_scope("pair"):
+        for i in range(TRI):
+            pair_step(i).wait_recv()
+            coef[z, block(i), :] = (
+                (sent[i].astype(F32) + other[i].astype(F32)) * scale
+            ).astype(BF16)
+            for way in range(2):
+                all_step(way, 0, i).start()
 
     def synthesised(t):
         got_all = lax.dot_general(
@@ -434,28 +456,34 @@
             rows[place, :] = chosen[:, s * LANES : (s + 1) * LANES]
 
     for step in range(1, far):
+      with jax.named_scope(f"all#s={step}"):
         for i in range(TRI):
             for way in range(2):
                 all_arrival(way, step - 1, i).wait_recv()
                 all_step(way, step, i).start()
+      with jax.named_scope(f"synth#s={step}"):
         if step == 1:
             synthesised(z)
         else:
             for way in ways:
                 synthesised(slot(-way * (step - 1)))
-    for way in ways:
-        synthesised(slot(-way * (far - 1)))
-    for i in range(TRI):
-        for way in range(2):
-            all_arrival(way, far - 1, i).wait_recv()
-    synthesised(slot(far))
-
-    for g in range(cons):
-        for s in range(2):
-            both = [
-                rows[pl.ds(s * ring * full + p * cons + g, ring, stride=full), :] for p in range(2)
-            ]
-            back[g, s] = jnp.concatenate(both, axis=0).astype(BF16)
+    with jax.named_scope("synth_last"):
+        for way in ways:
+            synthesised(slot(-way * (far - 1)))
+    with jax.named_scope("all_last"):
+        for i in range(TRI):
+            for way in range(2):
+                all_arrival(way, far - 1, i).wait_recv()
+    with jax.named_scope("synth_far"):
+        synthesised(slot(far))
+
+    with jax.named_scope("back"):
+        for g in range(cons):
+            for s in range(2):
+                both = [
+                    rows[pl.ds(s * ring * full + p * cons + g, ring, stride=full), :] for p in range(2)
+                ]
+                back[g, s] = jnp.concatenate(both, axis=0).astype(BF16)
 
     @pl.loop(1, peers)
     def _(offset):
@@ -470,36 +498,46 @@
                 sum_step(way, step, i).wait_send()
                 all_step(way, step, i).wait_send()
 
-    @pl.loop(1, peers)
-    def _(offset):
-        exchange(offset, back, returned, back_send, back_recv).wait()
+    with jax.named_scope("wait_back"):
+
+        @pl.loop(1, peers)
+        def _(offset):
+            exchange(offset, back, returned, back_send, back_recv).wait()
 
     out[...] = returned[...]
 
 
-def middle(pieces, legendre, love, assignment):
-    cons = pieces.shape[0]
+def middle(elevation, legendre, cycle_weight, love_factor, assignment):
+    cons = lax.axis_size("cons")
+    period = elevation.shape[-1]
     depth = legendre.shape[2]
     ring = 8
     far = ring // 2
     full = 2 * cons
     dma = pltpu.SemaphoreType.DMA
     vmem = pltpu.VMEM
+    twiddle, basis = phase_tables(period)
+    pieces = (cons, 2, 16, LANES)
     return pl.pallas_call(
         functools.partial(middle_kernel, ring, cons),
-        out_shape=jax.ShapeDtypeStruct(pieces.shape, BF16),
-        in_specs=[
-            pl.BlockSpec(memory_space=pltpu.VMEM),
-            pl.BlockSpec(memory_space=pl.ANY),
-            pl.BlockSpec(memory_space=pltpu.VMEM),
-            pl.BlockSpec(memory_space=pltpu.SMEM),
-        ],
+        out_shape=jax.ShapeDtypeStruct(pieces, BF16),
+        in_specs=[pl.BlockSpec(memory_space=pltpu.HBM)] * 7,
         out_specs=pl.BlockSpec(memory_space=pltpu.VMEM),
         scratch_shapes=[
+            vmem((1, CYC, period), BF16),
+            pltpu.SMEM((CYC,), F32),
+            vmem((depth,), F32),
+            pltpu.SMEM((cons,), jnp.int32),
+            vmem(twiddle.shape, F32),
+            vmem(basis.shape, BF16),
+            vmem(pieces, BF16),
+            vmem((CYC, period), F32),
+            vmem((RADIX // TRI * LANES, 2 * LANES), F32),
+            vmem((RADIX // TRI * full, LANES), F32),
             vmem((2, CYC, TRI * ring, depth), BF16),
             vmem((depth // LANES, CYC * TRI * ring, LANES), F32),
             vmem((ring, 2 * LANES, depth), BF16),
-            vmem(pieces.shape, BF16),
+            vmem(pieces, BF16),
             vmem((2 * cons * 16, LANES), F32),
             vmem((ring, full, 2 * LANES), F32),
             vmem((ring, TRI * full, depth), BF16),
@@ -510,8 +548,9 @@
             vmem((TRI, full, depth), BF16),
             vmem((ring, TRI * full, depth), BF16),
             vmem((2 * ring * full, LANES), F32),
-            vmem(pieces.shape, BF16),
-            vmem(pieces.shape, BF16),
+            vmem(pieces, BF16),
+            vmem(pieces, BF16),
+            dma((6,)),
             dma,
             dma,
             dma,
@@ -527,17 +566,22 @@
             dma((2 * cons,)),
         ],
         compiler_params=pltpu.CompilerParams(
-            collective_id=KERNEL_ID, has_side_effects=True, vmem_limit_bytes=50 * 2**20
+            collective_id=KERNEL_ID, has_side_effects=True, vmem_limit_bytes=67_000_000
         ),
         name="middle",
-    )(pieces, legendre, love, assignment)
+    )(
+        elevation,
+        legendre,
+        cycle_weight,
+        love_factor,
+        assignment,
+        jnp.asarray(twiddle),
+        jnp.asarray(basis),
+    )
 
 
 def local(elevation, legendre, cycle_weight, love_factor, assignment):
-    cons = lax.axis_size("cons")
-    lane_weight = jnp.pad(jnp.tile(cycle_weight, TRI), (0, LANES - TRI * CYC))[None, :]
-    pieces = forward(elevation, lane_weight, cons)
-    returned = middle(pieces, legendre, love_factor[None, :], assignment)
+    returned = middle(elevation, legendre, cycle_weight, love_factor, assignment)
     return inverse(returned, elevation.shape[-1])
 
 

time: 79.7 us -> 72 us (0.903)
  local copies, waits for them, and re-layouts: 6 us -> 1.7 us
  Pallas kernels: 73.4 us -> 70.1 us
    pallas_call x1 -> x0, Pallas kernels: 3.29 us -> none  [forward(): pl.pallas_call(forward_kernel, out_shape=jax.ShapeDtypeStruct((cons, 2, 1...]
    unnamed x8 -> x6, local copies, waits for them, and re-layouts: 4.03 us -> 1.7 us
    broadcast_in_dim x2 -> x0, local copies, waits for them, and re-layouts: 1.24 us -> none  [the longest x1 0.69 us: local(): returned = middle(pieces, legendre, love_factor[None, :], assignment)]
    pallas_call x1, Pallas kernels: 3.66 us -> 2.72 us  [inverse(): pl.pallas_call(inverse_kernel, out_shape=jax.ShapeDtypeStruct((1, CYC, pe...]
    pallas_call x1, Pallas kernels: 66.5 us -> 67.3 us  [middle(): pl.pallas_call(functools.partial(middle_kernel, ring, cons), out_shape=ja...]
where the time goes in v3:
time: 72 us; the launch traced here: 71.8 us
  Pallas kernels  70.1 us (97%)
  local copies, waits for them, and re-layouts  1.7 us (2%)
    pallas_call x1, Pallas kernels, middle(): pl.pallas_call(functools.partial(middle_kernel, ring, cons), out_shape=ja...  67.3 us
    pallas_call x1, Pallas kernels, inverse(): pl.pallas_call(inverse_kernel, out_shape=jax.ShapeDtypeStruct((1, CYC, pe...  2.72 us
    unnamed x6, local copies, waits for them, and re-layouts  1.7 us

profile of v3, /device:TPU:1, one launch (start us, length us, event | category | flops | bytes accessed | tf_op | source)
XLA Modules:
  0.0 71.8 jit_solution(5399807567664167071)
XLA Ops:
  0.0 0.0 copy-start.2
  0.0 67.3 %middle.1.z_ref = bf16[16,2,16,128]{3,2,1,0:T(8,128)(2,1)} custom-call(bf16[1,40,6144]{2,1,0:T(8,128)(2,1)} %elevation.1, bf16[40,48,768]{2,1,0:T(8,128)(2,1)} %legendre.1, f32[40]{0:T(128)} %cycle_weight.1, f32[768]{0:T(1024)} %love_factor.1, s32[16]{0:T(128)} %assigned.1, f32[96,128]{1,0:T(8,128)} %constant.4.clone.twiddles.twiddle_ref, ...), custom_call_target="tpu_custom_call" | custom-call | tf_op jit(solution)/shard_map/middle/pallas_call | solution.py:521
  67.3 0.0 copy-done.2
  67.4 0.0 copy-start
  67.4 0.9 %copy-done = bf16[16,2,16,128]{3,2,1,0:T(8,128)(2,1)S(1)} copy-done((bf16[16,2,16,128]{3,2,1,0:T(8,128)(2,1)S(1)}, bf16[16,2,16,128]{3,2,1,0:T(8,128)(2,1)}, u32[]{:S(2)}) %copy-start) | copy-done | bytes 131096
  68.3 0.0 copy-start.1
  68.3 0.8 %copy-done.1 = f32[96,128]{1,0:T(8,128)S(1)} copy-done((f32[96,128]{1,0:T(8,128)S(1)}, f32[96,128]{1,0:T(8,128)}, u32[]{:S(2)}) %copy-start.1) | copy-done | bytes 49176
  69.1 2.7 %inverse.1 = f32[1,40,6144]{2,1,0:T(8,128)} custom-call(bf16[16,2,16,128]{3,2,1,0:T(8,128)(2,1)S(1)} %copy-done, f32[96,128]{1,0:T(8,128)S(1)} %copy-done.1, bf16[32,256]{1,0:T(8,128)(2,1)S(1)} %copy-done.2), custom_call_target="tpu_custom_call" | custom-call | tf_op jit(solution)/shard_map/inverse/pallas_call | solution.py:182
Async XLA Ops:
  0.0 67.3 %copy-start.2 = (bf16[32,256]{1,0:T(8,128)(2,1)S(1)}, bf16[32,256]{1,0:T(8,128)(2,1)}, u32[]{:S(2)}) copy-start(bf16[32,256]{1,0:T(8,128)(2,1)} %constant.5.clone.bases.basis_ref) | copy-start | bytes 49156
  67.4 0.9 %copy-start = (bf16[16,2,16,128]{3,2,1,0:T(8,128)(2,1)S(1)}, bf16[16,2,16,128]{3,2,1,0:T(8,128)(2,1)}, u32[]{:S(2)}) copy-start(bf16[16,2,16,128]{3,2,1,0:T(8,128)(2,1)} %middle.1.z_ref) | copy-start | bytes 393220
  68.3 0.8 %copy-start.1 = (f32[96,128]{1,0:T(8,128)S(1)}, f32[96,128]{1,0:T(8,128)}, u32[]{:S(2)}) copy-start(f32[96,128]{1,0:T(8,128)} %constant.4.clone.twiddles.twiddle_ref) | copy-start | bytes 147460

commit v4 on v3

--- a/solution.py
+++ b/solution.py
@@ -104,18 +104,22 @@
     return twiddle.reshape(2 * RADIX, LANES).astype(np.float32), basis.astype(jnp.bfloat16)
 
 
-def transformed(x_ref, weight, twiddle_ref, basis_ref, out_ref, wide, mixed, rows):
+def transformed(x_ref, weight, twiddle_ref, basis_ref, out_ref, mixed, rows):
     cons = out_ref.shape[0]
     for triple in range(RADIX // TRI):
         mixed[triple * LANES + TRI * CYC : (triple + 1) * LANES, :] = jnp.zeros(
             (LANES - TRI * CYC, 2 * LANES), jnp.float32
         )
-    wide[...] = x_ref[...].reshape(wide.shape).astype(jnp.float32)
 
     @pl.loop(0, CYC // 8)
     def _(group):
         lines = pl.ds(pl.multiple_of(group * 8, 8), 8)
-        half = real_fft([wide[lines, k * LANES : (k + 1) * LANES] for k in range(RADIX)])
+        half = real_fft(
+            [
+                x_ref[0, lines, k * LANES : (k + 1) * LANES].astype(jnp.float32)
+                for k in range(RADIX)
+            ]
+        )
         for r in range(RADIX):
             re, im = at(half, r, RADIX)
             cos, sin = twiddle_ref[2 * r : 2 * r + 1, :], twiddle_ref[2 * r + 1 : 2 * r + 2, :]
@@ -142,7 +146,18 @@
             out_ref[c, h] = jnp.concatenate(both, axis=0).astype(jnp.bfloat16)
 
 
-def inverse_kernel(z_ref, twiddle_ref, basis_ref, out_ref, rows, mixed):
+def inverse_kernel(
+    z_hbm, twiddle_hbm, basis_hbm, out_hbm, z_ref, twiddle_ref, basis_ref, rows, mixed, done, sems, out_sems
+):
+    pairs = ((z_hbm, z_ref), (twiddle_hbm, twiddle_ref), (basis_hbm, basis_ref))
+    loads = [
+        pltpu.make_async_copy(source, target, sems.at[i])
+        for i, (source, target) in enumerate(pairs)
+    ]
+    for load in loads:
+        load.start()
+    for load in loads:
+        load.wait()
     cons = z_ref.shape[0]
     for c in range(cons):
         for h in range(2):
@@ -155,6 +170,10 @@
         mixed[triple * LANES : (triple + 1) * LANES, :] = jnp.dot(
             lines, basis_ref[...], preferred_element_type=jnp.float32
         )
+
+    def leave(group):
+        lines = pl.ds(pl.multiple_of(group * 8, 8), 8)
+        return pltpu.make_async_copy(done.at[group], out_hbm.at[0, lines], out_sems.at[group])
 
     @pl.loop(0, CYC // 8)
     def _(group):
@@ -171,9 +190,13 @@
             pair = plus(turned[r], conj(turned[RADIX - r]))
             half.append((pair[0] * np.float32(0.5), pair[1] * np.float32(0.5)))
         half.append((turned[middle][0], None))
-        lines = pl.ds(pl.multiple_of(group * 8, 8), 8)
         for k, value in enumerate(real_inverse(half, RADIX)):
-            out_ref[0, lines, k * LANES : (k + 1) * LANES] = value
+            done[group, :, k * LANES : (k + 1) * LANES] = value
+        leave(group).start()
+
+    @pl.loop(0, CYC // 8)
+    def _(group):
+        leave(group).wait()
 
 
 def inverse(pieces, period):
@@ -182,13 +205,19 @@
     return pl.pallas_call(
         inverse_kernel,
         out_shape=jax.ShapeDtypeStruct((1, CYC, period), jnp.float32),
-        in_specs=[pl.BlockSpec(memory_space=pltpu.VMEM)] * 3,
-        out_specs=pl.BlockSpec(memory_space=pltpu.VMEM),
+        in_specs=[pl.BlockSpec(memory_space=pltpu.HBM)] * 3,
+        out_specs=pl.BlockSpec(memory_space=pltpu.HBM),
         scratch_shapes=[
+            pltpu.VMEM(pieces.shape, jnp.bfloat16),
+            pltpu.VMEM(twiddle.shape, jnp.float32),
+            pltpu.VMEM(basis.shape, jnp.bfloat16),
             pltpu.VMEM((2 * cons * 16, LANES), jnp.float32),
             pltpu.VMEM((RADIX // TRI * LANES, 2 * LANES), jnp.float32),
+            pltpu.VMEM((CYC // 8, 8, period), jnp.float32),
+            pltpu.SemaphoreType.DMA((3,)),
+            pltpu.SemaphoreType.DMA((CYC // 8,)),
         ],
-        compiler_params=pltpu.CompilerParams(vmem_limit_bytes=10 * 2**20),
+        compiler_params=pltpu.CompilerParams(vmem_limit_bytes=67_000_000),
         name="inverse",
     )(pieces, jnp.asarray(twiddle), jnp.asarray(basis))
 
@@ -201,9 +230,9 @@
 
 def middle_kernel(
     ring, cons, elevation, legendre, cycle_weight, love_factor, assigned, twiddles, bases, out,
-    height, weights, love, assignment, twiddle, basis, pieces, tall, spun, spread,
+    height, weights, love, assignment, twiddle, basis, pieces, spun, spread,
     held, wide, table, got, mixed, lines, part, first, later, staged, sent, other, coef,
-    rows, back, returned,
+    rows, back,
     load_sem, own_sem, swap_send, swap_recv, out_send, out_recv, sum_send, sum_recv, pair_send, pair_recv,
     all_send, all_recv, back_send, back_recv,
 ):
@@ -230,6 +259,10 @@
         index = lax.rem(me + offset, peers)
         return index // 2, lax.rem(index, 2)
 
+    def outward(turn):
+        odd = lax.rem(turn, 2)
+        return peers // 2 + ((turn + 1) // 2) * (2 * odd - 1)
+
     def remote(source, target, send, recv, device):
         return pltpu.make_async_remote_copy(
             src_ref=source,
@@ -252,21 +285,10 @@
 
     across = (c, (1 - line) * 2 * ring + z * 2 + core)
 
-    @pl.loop(1, peers)
-    def _(offset):
-        there = peer(offset)
-        pl.semaphore_signal(
-            barrier, inc=1, device_id=(there[0], chip + there[1]), device_id_type=MESH
-        )
-
-    for target in (on_ring(1), on_ring(-1), across):
-        pl.semaphore_signal(barrier, inc=1, device_id=target, device_id_type=MESH)
-
     def half_of(which):
         return legendre.at[:, pl.ds(pl.multiple_of(which * half_orders, 8), half_orders), :]
 
     mine = pltpu.make_async_copy(half_of(core), held.at[core], own_sem)
-    mine.start()
     pairs = (
         (elevation, height),
         (twiddles, twiddle),
@@ -279,10 +301,23 @@
         pltpu.make_async_copy(source, target, load_sem.at[i])
         for i, (source, target) in enumerate(pairs)
     ]
-    for load in loads:
-        load.start()
-    for load in loads:
-        load.wait()
+    with jax.named_scope("signals"):
+        for load in loads:
+            load.start()
+
+        @pl.loop(0, peers - 1)
+        def _(turn):
+            there = peer(outward(turn))
+            pl.semaphore_signal(
+                barrier, inc=1, device_id=(there[0], chip + there[1]), device_id_type=MESH
+            )
+
+        for target in (on_ring(1), on_ring(-1), across):
+            pl.semaphore_signal(barrier, inc=1, device_id=target, device_id_type=MESH)
+        mine.start()
+    with jax.named_scope("loads"):
+        for load in loads:
+            load.wait()
 
     with jax.named_scope("fft"):
         lane_of = lax.broadcasted_iota(jnp.int32, (1, LANES), 1)
@@ -290,7 +325,7 @@
         weight = jnp.zeros((1, LANES), F32)
         for j in range(CYC):
             weight = jnp.where(day == j, weights[j], weight)
-        transformed(height, weight, twiddle, basis, pieces, tall, spun, spread)
+        transformed(height, weight, twiddle, basis, pieces, spun, spread)
 
     with jax.named_scope("barrier"):
         pl.semaphore_wait(barrier, peers + 2)
@@ -298,9 +333,9 @@
     swap = remote(half_of(1 - core), held.at[core], swap_send, swap_recv, (c, chip + 1 - core))
     swap.start()
 
-    @pl.loop(1, peers)
-    def _(offset):
-        exchange(offset, pieces, got, out_send, out_recv).start()
+    @pl.loop(0, peers - 1)
+    def _(turn):
+        exchange(outward(turn), pieces, got, out_send, out_recv).start()
 
     got[c, core] = pieces[c, core]
 
@@ -362,85 +397,90 @@
             jnp.concatenate(left, axis=0).astype(BF16), table[t], preferred_element_type=F32
         ).astype(BF16)
 
-    def block(i):
-        return pl.ds(i * full, full)
-
     def piece(i, p):
         return pl.ds(i * full + p * cons, cons)
 
     ways = (1, -1)
 
-    def sum_step(way, step, i):
+    def sum_step(way, step, i, p):
         device = on_ring(ways[way])
-        send, recv = sum_send.at[way, step, i], sum_recv.at[way, step, i]
+        send, recv = sum_send.at[way, step, i, p], sum_recv.at[way, step, i, p]
         if step == 0:
-            return remote(part.at[slot(far), piece(i, way)], first.at[way, i], send, recv, device)
-        return remote(staged.at[way, step - 1, i], later.at[way, step - 1, i], send, recv, device)
-
+            return remote(part.at[slot(far), piece(i, p)], first.at[way, i], send, recv, device)
+        landing = later.at[way, step - 1, i, p]
+        if step == 1 and p != way:
+            owner = slot(ways[way] * (far - 1))
+            return remote(part.at[owner, piece(i, p)], landing, send, recv, device)
+        return remote(staged.at[way, step - 1, i, p], landing, send, recv, device)
+
+    triples, ends = range(TRI), range(2)
     with jax.named_scope("first_part"):
         analysed(slot(far))
-        for i in range(TRI):
-            for way in range(2):
-                sum_step(way, 0, i).start()
+        for i in triples:
+            for way in ends:
+                sum_step(way, 0, i, way).start()
+        for way in ends:
+            analysed(slot(ways[way] * (far - 1)))
+            for i in triples:
+                sum_step(way, 1, i, 1 - way).start()
+        for way in ends:
+            analysed(slot(ways[way] * (far - 2)))
     for step in range(1, far):
-      with jax.named_scope(f"part#s={step}"):
-        for way in range(2):
-            analysed(slot(ways[way] * (far - step)))
-      with jax.named_scope(f"sum#s={step}"):
-        for i in range(TRI):
-            for way in range(2):
-                owner = slot(ways[way] * (far - step))
-                sum_step(way, step - 1, i).wait_recv()
-                if step == 1:
-                    for p in range(2):
-                        value = part[owner, piece(i, p), :]
-                        if p == way:
-                            value = (value.astype(F32) + first[way, i].astype(F32)).astype(BF16)
-                        staged[way, 0, i, p * cons : (p + 1) * cons, :] = value
-                else:
-                    staged[way, step - 1, i] = (
-                        part[owner, block(i), :].astype(F32) + later[way, step - 2, i].astype(F32)
-                    ).astype(BF16)
-                sum_step(way, step, i).start()
-    analysed(z)
-
-    def pair_step(i):
-        return remote(sent.at[i], other.at[i], pair_send.at[i], pair_recv.at[i], across)
+        with jax.named_scope(f"sum#s={step}"):
+            for late in ends:
+                for i in triples:
+                    for way in ends:
+                        p = way if late else 1 - way
+                        if step == 1 and not late:
+                            continue
+                        owner = slot(ways[way] * (far - step))
+                        sum_step(way, step - 1, i, p).wait_recv()
+                        come = first[way, i] if step == 1 else later[way, step - 2, i, p]
+                        staged[way, step - 1, i, p] = (
+                            part[owner, piece(i, p), :].astype(F32) + come.astype(F32)
+                        ).astype(BF16)
+                        sum_step(way, step, i, p).start()
+        if step == 1:
+            for way in ends:
+                analysed(slot(ways[way] * (far - 3)))
+        elif step == 2:
+            analysed(z)
+
+    def pair_step(i, p):
+        return remote(
+            sent.at[i, p], other.at[i, p], pair_send.at[i, p], pair_recv.at[i, p], across
+        )
 
     with jax.named_scope("last_sum"):
-        for i in range(TRI):
-            for way in range(2):
-                sum_step(way, far - 1, i).wait_recv()
-            sent[i] = (
-                part[z, block(i), :].astype(F32)
-                + later[0, far - 2, i].astype(F32)
-                + later[1, far - 2, i].astype(F32)
-            ).astype(BF16)
-            pair_step(i).start()
-
-    def all_step(way, step, i):
-        place = piece(i, way) if step == far - 1 else block(i)
-        ref = coef.at[slot(-ways[way] * step), place]
-        return remote(
-            ref, ref, all_send.at[way, step, i], all_recv.at[way, step, i], on_ring(ways[way])
-        )
-
-    def all_arrival(way, step, i):
-        place = piece(i, way) if step == far - 1 else block(i)
-        ref = coef.at[slot(-ways[way] * (step + 1)), place]
-        return remote(
-            ref, ref, all_send.at[way, step, i], all_recv.at[way, step, i], on_ring(ways[way])
-        )
-
-    scale = love[...].reshape(1, depth)
+        for i in triples:
+            for p in ends:
+                for way in ends:
+                    sum_step(way, far - 1, i, p).wait_recv()
+                sent[i, p] = (
+                    part[z, piece(i, p), :].astype(F32)
+                    + later[0, far - 2, i, p].astype(F32)
+                    + later[1, far - 2, i, p].astype(F32)
+                ).astype(BF16)
+                pair_step(i, p).start()
+
+    def all_step(way, step, i, p, late=0):
+        ref = coef.at[slot(-ways[way] * (step + late)), piece(i, p)]
+        send, recv = all_send.at[way, step, i, p], all_recv.at[way, step, i, p]
+        return remote(ref, ref, send, recv, on_ring(ways[way]))
+
+    def all_arrival(way, step, i, p):
+        return all_step(way, step, i, p, 1)
+
     with jax.named_scope("pair"):
-        for i in range(TRI):
-            pair_step(i).wait_recv()
-            coef[z, block(i), :] = (
-                (sent[i].astype(F32) + other[i].astype(F32)) * scale
-            ).astype(BF16)
-            for way in range(2):
-                all_step(way, 0, i).start()
+        scale = love[...].reshape(1, depth)
+        for i in triples:
+            for p in ends:
+                pair_step(i, p).wait_recv()
+                coef[z, piece(i, p), :] = (
+                    (sent[i, p].astype(F32) + other[i, p].astype(F32)) * scale
+                ).astype(BF16)
+                for way in ends:
+                    all_step(way, 0, i, p).start()
 
     def synthesised(t):
         got_all = lax.dot_general(
@@ -456,24 +496,26 @@
             rows[place, :] = chosen[:, s * LANES : (s + 1) * LANES]
 
     for step in range(1, far):
-      with jax.named_scope(f"all#s={step}"):
-        for i in range(TRI):
-            for way in range(2):
-                all_arrival(way, step - 1, i).wait_recv()
-                all_step(way, step, i).start()
-      with jax.named_scope(f"synth#s={step}"):
-        if step == 1:
-            synthesised(z)
-        else:
-            for way in ways:
-                synthesised(slot(-way * (step - 1)))
+        with jax.named_scope(f"all#s={step}"):
+            for i in triples:
+                for p in ends:
+                    for way in ends:
+                        all_arrival(way, step - 1, i, p).wait_recv()
+                        if step < far - 1 or p == way:
+                            all_step(way, step, i, p).start()
+        with jax.named_scope(f"synth#s={step}"):
+            if step == 1:
+                synthesised(z)
+            else:
+                for way in ways:
+                    synthesised(slot(-way * (step - 1)))
     with jax.named_scope("synth_last"):
         for way in ways:
             synthesised(slot(-way * (far - 1)))
     with jax.named_scope("all_last"):
-        for i in range(TRI):
-            for way in range(2):
-                all_arrival(way, far - 1, i).wait_recv()
+        for i in triples:
+            for way in ends:
+                all_arrival(way, far - 1, i, way).wait_recv()
     with jax.named_scope("synth_far"):
         synthesised(slot(far))
 
@@ -485,26 +527,30 @@
                 ]
                 back[g, s] = jnp.concatenate(both, axis=0).astype(BF16)
 
-    @pl.loop(1, peers)
-    def _(offset):
-        exchange(offset, back, returned, back_send, back_recv).start()
-
-    returned[c, core] = back[c, core]
-
-    for i in range(TRI):
-        pair_step(i).wait_send()
-        for way in range(2):
-            for step in range(far):
-                sum_step(way, step, i).wait_send()
-                all_step(way, step, i).wait_send()
+    @pl.loop(0, peers - 1)
+    def _(turn):
+        exchange(outward(turn), back, out, back_send, back_recv).start()
+
+    kept = pltpu.make_async_copy(back.at[c, core], out.at[c, core], own_sem)
+    kept.start()
+
+    with jax.named_scope("wait_sends"):
+        for i in triples:
+            for p in ends:
+                pair_step(i, p).wait_send()
+                for way in ends:
+                    for step in range(far):
+                        if step > 0 or p == way:
+                            sum_step(way, step, i, p).wait_send()
+                        if step < far - 1 or p == way:
+                            all_step(way, step, i, p).wait_send()
+        kept.wait()
 
     with jax.named_scope("wait_back"):
 
         @pl.loop(1, peers)
         def _(offset):
-            exchange(offset, back, returned, back_send, back_recv).wait()
-
-    out[...] = returned[...]
+            exchange(offset, back, out, back_send, back_recv).wait()
 
 
 def middle(elevation, legendre, cycle_weight, love_factor, assignment):
@@ -522,7 +568,7 @@
         functools.partial(middle_kernel, ring, cons),
         out_shape=jax.ShapeDtypeStruct(pieces, BF16),
         in_specs=[pl.BlockSpec(memory_space=pltpu.HBM)] * 7,
-        out_specs=pl.BlockSpec(memory_space=pltpu.VMEM),
+        out_specs=pl.BlockSpec(memory_space=pltpu.HBM),
         scratch_shapes=[
             vmem((1, CYC, period), BF16),
             pltpu.SMEM((CYC,), F32),
@@ -531,7 +577,6 @@
             vmem(twiddle.shape, F32),
             vmem(basis.shape, BF16),
             vmem(pieces, BF16),
-            vmem((CYC, period), F32),
             vmem((RADIX // TRI * LANES, 2 * LANES), F32),
             vmem((RADIX // TRI * full, LANES), F32),
             vmem((2, CYC, TRI * ring, depth), BF16),
@@ -542,13 +587,12 @@
             vmem((ring, full, 2 * LANES), F32),
             vmem((ring, TRI * full, depth), BF16),
             vmem((2, TRI, cons, depth), BF16),
-            vmem((2, far - 1, TRI, full, depth), BF16),
-            vmem((2, far - 1, TRI, full, depth), BF16),
-            vmem((TRI, full, depth), BF16),
-            vmem((TRI, full, depth), BF16),
+            vmem((2, far - 1, TRI, 2, cons, depth), BF16),
+            vmem((2, far - 1, TRI, 2, cons, depth), BF16),
+            vmem((TRI, 2, cons, depth), BF16),
+            vmem((TRI, 2, cons, depth), BF16),
             vmem((ring, TRI * full, depth), BF16),
             vmem((2 * ring * full, LANES), F32),
-            vmem(pieces, BF16),
             vmem(pieces, BF16),
             dma((6,)),
             dma,
@@ -556,12 +600,12 @@
             dma,
             dma((2 * cons,)),
             dma((2 * cons,)),
-            dma((2, far, TRI)),
-            dma((2, far, TRI)),
-            dma((TRI,)),
-            dma((TRI,)),
-            dma((2, far, TRI)),
-            dma((2, far, TRI)),
+            dma((2, far, TRI, 2)),
+            dma((2, far, TRI, 2)),
+            dma((TRI, 2)),
+            dma((TRI, 2)),
+            dma((2, far, TRI, 2)),
+            dma((2, far, TRI, 2)),
             dma((2 * cons,)),
             dma((2 * cons,)),
         ],

time: 72 us -> 67 us (0.931)
  Pallas kernels: 70.1 us -> 66.8 us
  local copies, waits for them, and re-layouts: 1.7 us -> 0 us
    pallas_call x1, Pallas kernels: 67.3 us -> 63.4 us  [middle(): pl.pallas_call(functools.partial(middle_kernel, ring, cons), out_shape=ja...]
    unnamed x6 -> x0, local copies, waits for them, and re-layouts: 1.7 us -> none
    pallas_call x1, Pallas kernels: 2.72 us -> 3.44 us  [inverse(): pl.pallas_call(inverse_kernel, out_shape=jax.ShapeDtypeStruct((1, CYC, pe...]
where the time goes in v4:
time: 67 us; the launch traced here: 66.9 us
  Pallas kernels  66.8 us (100%)
    pallas_call x1, Pallas kernels, middle(): pl.pallas_call(functools.partial(middle_kernel, ring, cons), out_shape=ja...  63.4 us
    pallas_call x1, Pallas kernels, inverse(): pl.pallas_call(inverse_kernel, out_shape=jax.ShapeDtypeStruct((1, CYC, pe...  3.44 us

profile of v4, /device:TPU:1, one launch (start us, length us, event | category | flops | bytes accessed | tf_op | source)
XLA Modules:
  0.0 66.9 jit_solution(11868540649221501655)
XLA Ops:
  0.0 63.4 %middle.1.z_hbm = bf16[16,2,16,128]{3,2,1,0:T(8,128)(2,1)} custom-call(bf16[1,40,6144]{2,1,0:T(8,128)(2,1)} %elevation.1, bf16[40,48,768]{2,1,0:T(8,128)(2,1)} %legendre.1, f32[40]{0:T(128)} %cycle_weight.1, f32[768]{0:T(1024)} %love_factor.1, s32[16]{0:T(128)} %assigned.1, f32[96,128]{1,0:T(8,128)} %constant.4.clone.twiddles.twiddle_hbm, ...), custom_call_target="tpu_custom_call" | custom-call | tf_op jit(solution)/shard_map/middle/pallas_call | solution.py:567
  63.4 3.4 %inverse.1 = f32[1,40,6144]{2,1,0:T(8,128)} custom-call(bf16[16,2,16,128]{3,2,1,0:T(8,128)(2,1)} %middle.1.z_hbm, f32[96,128]{1,0:T(8,128)} %constant.4.clone.twiddles.twiddle_hbm, bf16[32,256]{1,0:T(8,128)(2,1)} %constant.5.clone.bases.basis_hbm), custom_call_target="tpu_custom_call" | custom-call | tf_op jit(solution)/shard_map/inverse/pallas_call | solution.py:205

commit v5 on v4

--- a/solution.py
+++ b/solution.py
@@ -105,7 +105,7 @@
 
 
 def transformed(x_ref, weight, twiddle_ref, basis_ref, out_ref, mixed, rows):
-    cons = out_ref.shape[0]
+    cons = out_ref.shape[0] // 2
     for triple in range(RADIX // TRI):
         mixed[triple * LANES + TRI * CYC : (triple + 1) * LANES, :] = jnp.zeros(
             (LANES - TRI * CYC, 2 * LANES), jnp.float32
@@ -143,7 +143,7 @@
             both = [
                 rows[pl.ds(h * 16 * cons + p * cons + c, 8, stride=2 * cons), :] for p in range(2)
             ]
-            out_ref[c, h] = jnp.concatenate(both, axis=0).astype(jnp.bfloat16)
+            out_ref[2 * c + h] = jnp.concatenate(both, axis=0).astype(jnp.bfloat16)
 
 
 def inverse_kernel(
@@ -158,11 +158,9 @@
         load.start()
     for load in loads:
         load.wait()
-    cons = z_ref.shape[0]
-    for c in range(cons):
-        for h in range(2):
-            place = (2 * c + h) * 16
-            rows[place : place + 16, :] = z_ref[c, h].astype(jnp.float32)
+    cons = z_ref.shape[0] // 2
+    for source in range(2 * cons):
+        rows[source * 16 : (source + 1) * 16, :] = z_ref[source].astype(jnp.float32)
     for triple in range(RADIX // TRI):
         h, t = divmod(triple, 8)
         both = [rows[pl.ds(h * 16 + p * 8 + t, cons, stride=32), :] for p in range(2)]
@@ -200,7 +198,7 @@
 
 
 def inverse(pieces, period):
-    cons = pieces.shape[0]
+    cons = pieces.shape[0] // 2
     twiddle, basis = phase_tables(period)
     return pl.pallas_call(
         inverse_kernel,
@@ -233,8 +231,8 @@
     height, weights, love, assignment, twiddle, basis, pieces, spun, spread,
     held, wide, table, got, mixed, lines, part, first, later, staged, sent, other, coef,
     rows, back,
-    load_sem, own_sem, swap_send, swap_recv, out_send, out_recv, sum_send, sum_recv, pair_send, pair_recv,
-    all_send, all_recv, back_send, back_recv,
+    load_sem, own_sem, swap_send, swap_recv, out_send, out_recv, sum_send, pair_send, all_send,
+    ring_recv, pair_recv, back_send, back_recv,
 ):
     c, b = lax.axis_index("cons"), lax.axis_index("blk")
     core = lax.rem(b, 2)
@@ -255,10 +253,6 @@
     def on_ring(offset):
         return (c, line * 2 * ring + slot(offset) * 2 + core)
 
-    def peer(offset):
-        index = lax.rem(me + offset, peers)
-        return index // 2, lax.rem(index, 2)
-
     def outward(turn):
         odd = lax.rem(turn, 2)
         return peers // 2 + ((turn + 1) // 2) * (2 * odd - 1)
@@ -274,14 +268,13 @@
         )
 
     def exchange(offset, source, landing, send, recv):
-        there = peer(offset)
-        return remote(
-            source.at[there[0], there[1]],
-            landing.at[c, core],
-            send.at[offset],
-            recv.at[offset],
-            (there[0], chip + there[1]),
-        )
+        index = lax.rem(me + offset, peers)
+        there = (index // 2, chip + lax.rem(index, 2))
+        return remote(source.at[index], landing.at[me], send, recv, there)
+
+    def exchanged(source, landing, send, recv):
+        rest = pl.ds(0, peers - 1)
+        return remote(source.at[rest], landing.at[rest], send, recv, (c, chip + 1 - core))
 
     across = (c, (1 - line) * 2 * ring + z * 2 + core)
 
@@ -307,10 +300,9 @@
 
         @pl.loop(0, peers - 1)
         def _(turn):
-            there = peer(outward(turn))
-            pl.semaphore_signal(
-                barrier, inc=1, device_id=(there[0], chip + there[1]), device_id_type=MESH
-            )
+            index = lax.rem(me + outward(turn), peers)
+            there = (index // 2, chip + lax.rem(index, 2))
+            pl.semaphore_signal(barrier, inc=1, device_id=there, device_id_type=MESH)
 
         for target in (on_ring(1), on_ring(-1), across):
             pl.semaphore_signal(barrier, inc=1, device_id=target, device_id_type=MESH)
@@ -337,7 +329,7 @@
     def _(turn):
         exchange(outward(turn), pieces, got, out_send, out_recv).start()
 
-    got[c, core] = pieces[c, core]
+    got[me] = pieces[me]
 
     def turn(which):
         @pl.loop(0, CYC)
@@ -369,16 +361,13 @@
         turn(1 - core)
 
     with jax.named_scope("wait_out"):
-
-        @pl.loop(1, peers)
-        def _(offset):
-            exchange(offset, pieces, got, out_send, out_recv).wait()
+        exchanged(pieces, got, out_send, out_recv).wait()
 
     with jax.named_scope("lines"):
         for g in range(cons):
             field = assignment[g]
             for s in range(2):
-                mixed[(s * cons + g) * 16 : (s * cons + g + 1) * 16, :] = got[field, s].astype(F32)
+                mixed[(s * cons + g) * 16 : (s * cons + g + 1) * 16, :] = got[2 * field + s].astype(F32)
         for t in range(ring):
             for s in range(2):
                 for p in range(2):
@@ -404,7 +393,7 @@
 
     def sum_step(way, step, i, p):
         device = on_ring(ways[way])
-        send, recv = sum_send.at[way, step, i, p], sum_recv.at[way, step, i, p]
+        send, recv = sum_send, ring_recv.at[way, step, i, p]
         if step == 0:
             return remote(part.at[slot(far), piece(i, p)], first.at[way, i], send, recv, device)
         landing = later.at[way, step - 1, i, p]
@@ -448,7 +437,7 @@
 
     def pair_step(i, p):
         return remote(
-            sent.at[i, p], other.at[i, p], pair_send.at[i, p], pair_recv.at[i, p], across
+            sent.at[i, p], other.at[i, p], pair_send, pair_recv.at[i, p], across
         )
 
     with jax.named_scope("last_sum"):
@@ -465,8 +454,7 @@
 
     def all_step(way, step, i, p, late=0):
         ref = coef.at[slot(-ways[way] * (step + late)), piece(i, p)]
-        send, recv = all_send.at[way, step, i, p], all_recv.at[way, step, i, p]
-        return remote(ref, ref, send, recv, on_ring(ways[way]))
+        return remote(ref, ref, all_send, ring_recv.at[way, step, i, p], on_ring(ways[way]))
 
     def all_arrival(way, step, i, p):
         return all_step(way, step, i, p, 1)
@@ -525,32 +513,24 @@
                 both = [
                     rows[pl.ds(s * ring * full + p * cons + g, ring, stride=full), :] for p in range(2)
                 ]
-                back[g, s] = jnp.concatenate(both, axis=0).astype(BF16)
+                back[2 * g + s] = jnp.concatenate(both, axis=0).astype(BF16)
 
     @pl.loop(0, peers - 1)
     def _(turn):
         exchange(outward(turn), back, out, back_send, back_recv).start()
 
-    kept = pltpu.make_async_copy(back.at[c, core], out.at[c, core], own_sem)
+    kept = pltpu.make_async_copy(back.at[me], out.at[me], own_sem)
     kept.start()
 
     with jax.named_scope("wait_sends"):
-        for i in triples:
-            for p in ends:
-                pair_step(i, p).wait_send()
-                for way in ends:
-                    for step in range(far):
-                        if step > 0 or p == way:
-                            sum_step(way, step, i, p).wait_send()
-                        if step < far - 1 or p == way:
-                            all_step(way, step, i, p).wait_send()
+        most = pl.ds(0, ring - 1)
+        remote(part.at[most], part.at[most], sum_send, own_sem, across).wait_send()
+        remote(coef.at[most], coef.at[most], all_send, own_sem, across).wait_send()
+        remote(sent, other, pair_send, own_sem, across).wait_send()
         kept.wait()
 
     with jax.named_scope("wait_back"):
-
-        @pl.loop(1, peers)
-        def _(offset):
-            exchange(offset, back, out, back_send, back_recv).wait()
+        exchanged(back, out, back_send, back_recv).wait()
 
 
 def middle(elevation, legendre, cycle_weight, love_factor, assignment):
@@ -563,7 +543,7 @@
     dma = pltpu.SemaphoreType.DMA
     vmem = pltpu.VMEM
     twiddle, basis = phase_tables(period)
-    pieces = (cons, 2, 16, LANES)
+    pieces = (2 * cons, 16, LANES)
     return pl.pallas_call(
         functools.partial(middle_kernel, ring, cons),
         out_shape=jax.ShapeDtypeStruct(pieces, BF16),
@@ -598,16 +578,15 @@
             dma,
             dma,
             dma,
-            dma((2 * cons,)),
-            dma((2 * cons,)),
-            dma((2, far, TRI, 2)),
+            dma,
+            dma,
+            dma,
+            dma,
+            dma,
             dma((2, far, TRI, 2)),
             dma((TRI, 2)),
-            dma((TRI, 2)),
-            dma((2, far, TRI, 2)),
-            dma((2, far, TRI, 2)),
-            dma((2 * cons,)),
-            dma((2 * cons,)),
+            dma,
+            dma,
         ],
         compiler_params=pltpu.CompilerParams(
             collective_id=KERNEL_ID, has_side_effects=True, vmem_limit_bytes=67_000_000

time: 67 us -> 64.5 us (0.963)
  Pallas kernels: 66.8 us -> 64.3 us
    pallas_call x1, Pallas kernels: 63.4 us -> 60.9 us  [middle(): pl.pallas_call(functools.partial(middle_kernel, ring, cons), out_shape=ja...]
where the time goes in v5:
time: 64.5 us; the launch traced here: 64.4 us
  Pallas kernels  64.3 us (100%)
    pallas_call x1, Pallas kernels, middle(): pl.pallas_call(functools.partial(middle_kernel, ring, cons), out_shape=ja...  60.9 us
    pallas_call x1, Pallas kernels, inverse(): pl.pallas_call(inverse_kernel, out_shape=jax.ShapeDtypeStruct((1, CYC, pe...  3.45 us

profile of v5, /device:TPU:1, one launch (start us, length us, event | category | flops | bytes accessed | tf_op | source)
XLA Modules:
  0.0 64.4 jit_solution(13467857032105119487)
XLA Ops:
  0.0 60.9 %middle.1.z_hbm = bf16[32,16,128]{2,1,0:T(8,128)(2,1)} custom-call(bf16[1,40,6144]{2,1,0:T(8,128)(2,1)} %elevation.1, bf16[40,48,768]{2,1,0:T(8,128)(2,1)} %legendre.1, f32[40]{0:T(128)} %cycle_weight.1, f32[768]{0:T(1024)} %love_factor.1, s32[16]{0:T(128)} %assigned.1, f32[96,128]{1,0:T(8,128)} %constant.4.clone.twiddles.twiddle_hbm, ...), custom_call_target="tpu_custom_call" | custom-call | tf_op jit(solution)/shard_map/middle/pallas_call | solution.py:547
  60.9 3.4 %inverse.1 = f32[1,40,6144]{2,1,0:T(8,128)} custom-call(bf16[32,16,128]{2,1,0:T(8,128)(2,1)} %middle.1.z_hbm, f32[96,128]{1,0:T(8,128)} %constant.4.clone.twiddles.twiddle_hbm, bf16[32,256]{1,0:T(8,128)(2,1)} %constant.5.clone.bases.basis_hbm), custom_call_target="tpu_custom_call" | custom-call | tf_op jit(solution)/shard_map/inverse/pallas_call | solution.py:203

commit v6 on v5

--- a/solution.py
+++ b/solution.py
@@ -229,10 +229,10 @@
 def middle_kernel(
     ring, cons, elevation, legendre, cycle_weight, love_factor, assigned, twiddles, bases, out,
     height, weights, love, assignment, twiddle, basis, pieces, spun, spread,
-    held, wide, table, got, mixed, lines, part, first, later, staged, sent, other, coef,
+    held, wide, table, got, mixed, lines, part, first, later, staged, sent, other, crossed, coef,
     rows, back,
     load_sem, own_sem, swap_send, swap_recv, out_send, out_recv, sum_send, pair_send, all_send,
-    ring_recv, pair_recv, back_send, back_recv,
+    ring_recv, pair_recv, cross_recv, back_send, back_recv,
 ):
     c, b = lax.axis_index("cons"), lax.axis_index("blk")
     core = lax.rem(b, 2)
@@ -304,7 +304,7 @@
             there = (index // 2, chip + lax.rem(index, 2))
             pl.semaphore_signal(barrier, inc=1, device_id=there, device_id_type=MESH)
 
-        for target in (on_ring(1), on_ring(-1), across):
+        for target in (on_ring(1), on_ring(-1), on_ring(2), on_ring(-2), across):
             pl.semaphore_signal(barrier, inc=1, device_id=target, device_id_type=MESH)
         mine.start()
     with jax.named_scope("loads"):
@@ -320,7 +320,7 @@
         transformed(height, weight, twiddle, basis, pieces, spun, spread)
 
     with jax.named_scope("barrier"):
-        pl.semaphore_wait(barrier, peers + 2)
+        pl.semaphore_wait(barrier, peers + 4)
 
     swap = remote(half_of(1 - core), held.at[core], swap_send, swap_recv, (c, chip + 1 - core))
     swap.start()
@@ -387,95 +387,19 @@
         ).astype(BF16)
 
     def piece(i, p):
-        return pl.ds(i * full + p * cons, cons)
-
-    ways = (1, -1)
-
-    def sum_step(way, step, i, p):
-        device = on_ring(ways[way])
-        send, recv = sum_send, ring_recv.at[way, step, i, p]
-        if step == 0:
-            return remote(part.at[slot(far), piece(i, p)], first.at[way, i], send, recv, device)
-        landing = later.at[way, step - 1, i, p]
-        if step == 1 and p != way:
-            owner = slot(ways[way] * (far - 1))
-            return remote(part.at[owner, piece(i, p)], landing, send, recv, device)
-        return remote(staged.at[way, step - 1, i, p], landing, send, recv, device)
-
-    triples, ends = range(TRI), range(2)
-    with jax.named_scope("first_part"):
-        analysed(slot(far))
-        for i in triples:
-            for way in ends:
-                sum_step(way, 0, i, way).start()
-        for way in ends:
-            analysed(slot(ways[way] * (far - 1)))
-            for i in triples:
-                sum_step(way, 1, i, 1 - way).start()
-        for way in ends:
-            analysed(slot(ways[way] * (far - 2)))
-    for step in range(1, far):
-        with jax.named_scope(f"sum#s={step}"):
-            for late in ends:
-                for i in triples:
-                    for way in ends:
-                        p = way if late else 1 - way
-                        if step == 1 and not late:
-                            continue
-                        owner = slot(ways[way] * (far - step))
-                        sum_step(way, step - 1, i, p).wait_recv()
-                        come = first[way, i] if step == 1 else later[way, step - 2, i, p]
-                        staged[way, step - 1, i, p] = (
-                            part[owner, piece(i, p), :].astype(F32) + come.astype(F32)
-                        ).astype(BF16)
-                        sum_step(way, step, i, p).start()
-        if step == 1:
-            for way in ends:
-                analysed(slot(ways[way] * (far - 3)))
-        elif step == 2:
-            analysed(z)
-
-    def pair_step(i, p):
-        return remote(
-            sent.at[i, p], other.at[i, p], pair_send, pair_recv.at[i, p], across
-        )
-
-    with jax.named_scope("last_sum"):
-        for i in triples:
-            for p in ends:
-                for way in ends:
-                    sum_step(way, far - 1, i, p).wait_recv()
-                sent[i, p] = (
-                    part[z, piece(i, p), :].astype(F32)
-                    + later[0, far - 2, i, p].astype(F32)
-                    + later[1, far - 2, i, p].astype(F32)
-                ).astype(BF16)
-                pair_step(i, p).start()
-
-    def all_step(way, step, i, p, late=0):
-        ref = coef.at[slot(-ways[way] * (step + late)), piece(i, p)]
-        return remote(ref, ref, all_send, ring_recv.at[way, step, i, p], on_ring(ways[way]))
-
-    def all_arrival(way, step, i, p):
-        return all_step(way, step, i, p, 1)
-
-    with jax.named_scope("pair"):
-        scale = love[...].reshape(1, depth)
-        for i in triples:
-            for p in ends:
-                pair_step(i, p).wait_recv()
-                coef[z, piece(i, p), :] = (
-                    (sent[i, p].astype(F32) + other[i, p].astype(F32)) * scale
-                ).astype(BF16)
-                for way in ends:
-                    all_step(way, 0, i, p).start()
+        return pl.ds(pl.multiple_of(i * full + p * cons, cons), cons)
+
+    ways, triples, ends = (1, -1), range(TRI), range(2)
+    scale = love[...].reshape(1, depth)
 
     def synthesised(t):
         got_all = lax.dot_general(
             coef[t], table[t], (((1,), (1,)), ((), ())), preferred_element_type=F32
         )
         chosen = jnp.where(
-            which == 0, got_all[:full], jnp.where(which == 1, got_all[full : 2 * full], got_all[2 * full :])
+            which == 0,
+            got_all[:full],
+            jnp.where(which == 1, got_all[full : 2 * full], got_all[2 * full :]),
         )
         order = which + (TRI * t + core * half_orders + c * 2 * half_orders)
         chosen = chosen * jnp.where(order == 0, 1.0, 2.0).astype(F32)
@@ -483,29 +407,237 @@
             place = pl.ds(pl.multiple_of(s * ring * full + t * full, 8), full)
             rows[place, :] = chosen[:, s * LANES : (s + 1) * LANES]
 
-    for step in range(1, far):
-        with jax.named_scope(f"all#s={step}"):
+    def sum_sent(source, target, way, step, i, p, hops=1):
+        return remote(
+            source, target, sum_send, ring_recv.at[way, step, i, p], on_ring(hops * ways[way])
+        )
+
+    @pl.when(core == 0)
+    def _():
+        def sum_step(way, step, i, p):
+            if step == 0:
+                source = part.at[slot(far), piece(i, p)]
+                return sum_sent(source, first.at[way, i], way, step, i, p, 2)
+            target = later.at[way, step - 1, i, p]
+            if step == 1:
+                source = part.at[slot(ways[way] * (far - 1)), piece(i, p)]
+            else:
+                source = staged.at[way, step - 1, i, p]
+            return sum_sent(source, target, way, step, i, p)
+
+        with jax.named_scope("first_part"):
+            analysed(slot(far))
+            for i in triples:
+                for way in ends:
+                    sum_step(way, 0, i, way).start()
+            for way in ends:
+                analysed(slot(ways[way] * (far - 1)))
+                for i in triples:
+                    for p in (1 - way, way):
+                        sum_step(way, 1, i, p).start()
+            for step in range(2, far):
+                for way in ends:
+                    analysed(slot(ways[way] * (far - step)))
+            analysed(z)
+        for step in range(2, far):
+            with jax.named_scope(f"sum#s={step}"):
+                for i in triples:
+                    for late in ends:
+                        for way in ends:
+                            p = way if late else 1 - way
+                            owner = slot(ways[way] * (far - step))
+                            sum_step(way, step - 1, i, p).wait_recv()
+                            total = part[owner, piece(i, p), :].astype(F32) + later[
+                                way, step - 2, i, p
+                            ].astype(F32)
+                            if step == 2 and late:
+                                sum_step(way, 0, i, p).wait_recv()
+                                total = total + first[way, i].astype(F32)
+                            staged[way, step - 1, i, p] = total.astype(BF16)
+                            sum_step(way, step, i, p).start()
+
+        def pair_step(i, p):
+            return remote(
+                sent.at[i, p], other.at[i, p], pair_send, pair_recv.at[i, p], across
+            )
+
+        with jax.named_scope("last_sum"):
             for i in triples:
                 for p in ends:
                     for way in ends:
-                        all_arrival(way, step - 1, i, p).wait_recv()
-                        if step < far - 1 or p == way:
+                        sum_step(way, far - 1, i, p).wait_recv()
+                    sent[i, p] = (
+                        part[z, piece(i, p), :].astype(F32)
+                        + later[0, far - 2, i, p].astype(F32)
+                        + later[1, far - 2, i, p].astype(F32)
+                    ).astype(BF16)
+                    pair_step(i, p).start()
+
+        def all_step(way, step, i, p, late=0):
+            hops = 2 if step == far else 1
+            distance = far - 2 if step == far else step
+            distance = distance + late * hops
+            ref = coef.at[slot(-ways[way] * distance), piece(i, p)]
+            return remote(
+                ref, ref, all_send, ring_recv.at[way, step, i, p], on_ring(hops * ways[way])
+            )
+
+        with jax.named_scope("pair"):
+            for i in triples:
+                for p in ends:
+                    pair_step(i, p).wait_recv()
+                    coef[z, piece(i, p), :] = (
+                        (sent[i, p].astype(F32) + other[i, p].astype(F32)) * scale
+                    ).astype(BF16)
+                    for way in ends:
+                        all_step(way, 0, i, p).start()
+        for step in range(1, far - 1):
+            with jax.named_scope(f"all#s={step}"):
+                for i in triples:
+                    for p in ends:
+                        for way in ends:
+                            all_step(way, step - 1, i, p, 1).wait_recv()
                             all_step(way, step, i, p).start()
-        with jax.named_scope(f"synth#s={step}"):
-            if step == 1:
-                synthesised(z)
-            else:
+                            if step == far - 2 and p == way:
+                                all_step(way, far, i, p).start()
+            with jax.named_scope(f"synth#s={step}"):
+                for owner in (0,) if step == 1 else (step - 1, 1 - step):
+                    synthesised(slot(owner))
+        with jax.named_scope("synth_last"):
+            for owner in (far - 2, 2 - far):
+                synthesised(slot(owner))
+        with jax.named_scope("all_last"):
+            for i in triples:
+                for p in ends:
+                    for way in ends:
+                        all_step(way, far - 2, i, p, 1).wait_recv()
+            for owner in (far - 1, 1 - far):
+                synthesised(slot(owner))
+            for i in triples:
+                for way in ends:
+                    all_step(way, far, i, way, 1).wait_recv()
+        with jax.named_scope("synth_far"):
+            synthesised(slot(far))
+        most = pl.ds(0, ring - 1)
+        remote(part.at[most], part.at[most], sum_send, own_sem, across).wait_send()
+        remote(coef.at[most], coef.at[most], all_send, own_sem, across).wait_send()
+        remote(sent, other, pair_send, own_sem, across).wait_send()
+
+    @pl.when(core == 1)
+    def _():
+        owners = [far]
+        for distance in range(far - 1, 0, -1):
+            owners += [distance, -distance]
+        owners.append(0)
+
+        def mixed_sum(owner, i):
+            k = owners.index(owner)
+            return part[slot(owner), piece(i, line), :].astype(F32) + crossed[k, i].astype(F32)
+
+        def taken(owner, turn):
+            k = owners.index(owner)
+            remote(
+                crossed.at[k], crossed.at[k], pair_send, cross_recv.at[turn, k], across
+            ).wait_recv()
+
+        def sum_step(way, step, i):
+            if step == 0:
+                return sum_sent(sent.at[i, 0], first.at[way, i], way, 0, i, 0)
+            source, target = staged.at[way, step - 1, i, 0], later.at[way, step - 1, i, 0]
+            return sum_sent(source, target, way, step, i, 0)
+
+        with jax.named_scope("first_part"):
+            for k, owner in enumerate(owners):
+                analysed(slot(owner))
+                for i in triples:
+                    remote(
+                        part.at[slot(owner), piece(i, 1 - line)],
+                        crossed.at[k, i],
+                        pair_send,
+                        cross_recv.at[0, k],
+                        across,
+                    ).start()
+        with jax.named_scope("sum#s=0"):
+            taken(far, 0)
+            for i in triples:
+                sent[i, 0] = mixed_sum(far, i).astype(BF16)
+                sum_step(i % 2, 0, i).start()
+        for step in range(1, far):
+            with jax.named_scope(f"sum#s={step}"):
+                for way in ends:
+                    taken(ways[way] * (far - step), 0)
+                for late in ends:
+                    for i in triples:
+                        for way in ends:
+                            if late != (way == i % 2):
+                                continue
+                            total = mixed_sum(ways[way] * (far - step), i)
+                            if step > 1 or late:
+                                sum_step(way, step - 1, i).wait_recv()
+                                come = first[way, i] if step == 1 else later[way, step - 2, i, 0]
+                                total = total + come.astype(F32)
+                            staged[way, step - 1, i, 0] = total.astype(BF16)
+                            sum_step(way, step, i).start()
+
+        def all_step(way, step, i, late=0):
+            ref = coef.at[slot(-ways[way] * (step + late)), piece(i, line)]
+            return remote(
+                ref, ref, all_send, ring_recv.at[way, step, i, 0], on_ring(ways[way])
+            )
+
+        def shared(owner, i):
+            ref = coef.at[slot(owner), piece(i, line)]
+            k = owners.index(owner)
+            return remote(ref, ref, pair_send, cross_recv.at[1, k], across)
+
+        with jax.named_scope("last_sum"):
+            taken(0, 0)
+            for i in triples:
+                for way in ends:
+                    sum_step(way, far - 1, i).wait_recv()
+                coef[z, piece(i, line), :] = (
+                    (
+                        mixed_sum(0, i)
+                        + later[0, far - 2, i, 0].astype(F32)
+                        + later[1, far - 2, i, 0].astype(F32)
+                    )
+                    * scale
+                ).astype(BF16)
+                for way in ends:
+                    all_step(way, 0, i).start()
+                shared(0, i).start()
+
+        def ended(owner):
+            taken(owner, 1)
+            synthesised(slot(owner))
+
+        for step in range(1, far):
+            with jax.named_scope(f"all#s={step}"):
+                for i in triples:
+                    for way in ends:
+                        all_step(way, step - 1, i, 1).wait_recv()
+                        if step < far - 1 or way == i % 2:
+                            all_step(way, step, i).start()
+                        shared(-ways[way] * step, i).start()
+            with jax.named_scope(f"synth#s={step}"):
+                if step == 2:
+                    ended(0)
+                elif step == 3:
+                    for way in ways:
+                        ended(way)
+        with jax.named_scope("all_last"):
+            for i in triples:
+                all_step(i % 2, far - 1, i, 1).wait_recv()
+                shared(far, i).start()
+        with jax.named_scope("synth_last"):
+            for distance in range(2, far):
                 for way in ways:
-                    synthesised(slot(-way * (step - 1)))
-    with jax.named_scope("synth_last"):
-        for way in ways:
-            synthesised(slot(-way * (far - 1)))
-    with jax.named_scope("all_last"):
-        for i in triples:
-            for way in ends:
-                all_arrival(way, far - 1, i, way).wait_recv()
-    with jax.named_scope("synth_far"):
-        synthesised(slot(far))
+                    ended(way * distance)
+            ended(far)
+        most = pl.ds(0, ring - 1)
+        remote(crossed.at[most], crossed.at[most], sum_send, own_sem, across).wait_send()
+        remote(crossed.at[most], crossed.at[most], all_send, own_sem, across).wait_send()
+        remote(coef, coef, pair_send, own_sem, across).wait_send()
 
     with jax.named_scope("back"):
         for g in range(cons):
@@ -523,10 +655,6 @@
     kept.start()
 
     with jax.named_scope("wait_sends"):
-        most = pl.ds(0, ring - 1)
-        remote(part.at[most], part.at[most], sum_send, own_sem, across).wait_send()
-        remote(coef.at[most], coef.at[most], all_send, own_sem, across).wait_send()
-        remote(sent, other, pair_send, own_sem, across).wait_send()
         kept.wait()
 
     with jax.named_scope("wait_back"):
@@ -571,6 +699,7 @@
             vmem((2, far - 1, TRI, 2, cons, depth), BF16),
             vmem((TRI, 2, cons, depth), BF16),
             vmem((TRI, 2, cons, depth), BF16),
+            vmem((ring, TRI, cons, depth), BF16),
             vmem((ring, TRI * full, depth), BF16),
             vmem((2 * ring * full, LANES), F32),
             vmem(pieces, BF16),
@@ -583,8 +712,9 @@
             dma,
             dma,
             dma,
-            dma((2, far, TRI, 2)),
+            dma((2, far + 1, TRI, 2)),
             dma((TRI, 2)),
+            dma((2, ring)),
             dma,
             dma,
         ],

time: 64.5 us -> 61.9 us (0.960)
  Pallas kernels: 64.3 us -> 61.8 us
    pallas_call x1, Pallas kernels: 60.9 us -> 58.3 us  [middle(): pl.pallas_call(functools.partial(middle_kernel, ring, cons), out_shape=ja...]
where the time goes in v6:
time: 61.9 us; the launch traced here: 61.8 us
  Pallas kernels  61.8 us (100%)
    pallas_call x1, Pallas kernels, middle(): pl.pallas_call(functools.partial(middle_kernel, ring, cons), out_shape=ja...  58.3 us
    pallas_call x1, Pallas kernels, inverse(): pl.pallas_call(inverse_kernel, out_shape=jax.ShapeDtypeStruct((1, CYC, pe...  3.44 us

profile of v6, /device:TPU:1, one launch (start us, length us, event | category | flops | bytes accessed | tf_op | source)
XLA Modules:
  0.0 61.8 jit_solution(13221197218153685118)
XLA Ops:
  0.0 58.3 %middle.1.z_hbm = bf16[32,16,128]{2,1,0:T(8,128)(2,1)} custom-call(bf16[1,40,6144]{2,1,0:T(8,128)(2,1)} %elevation.1, bf16[40,48,768]{2,1,0:T(8,128)(2,1)} %legendre.1, f32[40]{0:T(128)} %cycle_weight.1, f32[768]{0:T(1024)} %love_factor.1, s32[16]{0:T(128)} %assigned.1, f32[96,128]{1,0:T(8,128)} %constant.4.clone.twiddles.twiddle_hbm, ...), custom_call_target="tpu_custom_call" | custom-call | tf_op jit(solution)/shard_map/middle/pallas_call | solution.py:675
  58.3 3.4 %inverse.1 = f32[1,40,6144]{2,1,0:T(8,128)} custom-call(bf16[32,16,128]{2,1,0:T(8,128)(2,1)} %middle.1.z_hbm, f32[96,128]{1,0:T(8,128)} %constant.4.clone.twiddles.twiddle_hbm, bf16[32,256]{1,0:T(8,128)(2,1)} %constant.5.clone.bases.basis_hbm), custom_call_target="tpu_custom_call" | custom-call | tf_op jit(solution)/shard_map/inverse/pallas_call | solution.py:203

commit v7 on v6

--- a/solution.py
+++ b/solution.py
@@ -231,8 +231,8 @@
     height, weights, love, assignment, twiddle, basis, pieces, spun, spread,
     held, wide, table, got, mixed, lines, part, first, later, staged, sent, other, crossed, coef,
     rows, back,
-    load_sem, own_sem, swap_send, swap_recv, out_send, out_recv, sum_send, pair_send, all_send,
-    ring_recv, pair_recv, cross_recv, back_send, back_recv,
+    own_sem, swap_send, swap_recv, out_send, out_recv, sum_send, pair_send, all_send,
+    ring_recv, cross_recv, back_send, back_recv,
 ):
     c, b = lax.axis_index("cons"), lax.axis_index("blk")
     core = lax.rem(b, 2)
@@ -253,9 +253,7 @@
     def on_ring(offset):
         return (c, line * 2 * ring + slot(offset) * 2 + core)
 
-    def outward(turn):
-        odd = lax.rem(turn, 2)
-        return peers // 2 + ((turn + 1) // 2) * (2 * odd - 1)
+    outward = sorted(range(1, peers), key=lambda offset: abs(offset - peers // 2))
 
     def remote(source, target, send, recv, device):
         return pltpu.make_async_remote_copy(
@@ -291,16 +289,15 @@
         (love_factor, love),
     )
     loads = [
-        pltpu.make_async_copy(source, target, load_sem.at[i])
+        pltpu.make_async_copy(source, target, cross_recv.at[1, i])
         for i, (source, target) in enumerate(pairs)
     ]
     with jax.named_scope("signals"):
         for load in loads:
             load.start()
 
-        @pl.loop(0, peers - 1)
-        def _(turn):
-            index = lax.rem(me + outward(turn), peers)
+        for offset in outward:
+            index = lax.rem(me + offset, peers)
             there = (index // 2, chip + lax.rem(index, 2))
             pl.semaphore_signal(barrier, inc=1, device_id=there, device_id_type=MESH)
 
@@ -325,9 +322,8 @@
     swap = remote(half_of(1 - core), held.at[core], swap_send, swap_recv, (c, chip + 1 - core))
     swap.start()
 
-    @pl.loop(0, peers - 1)
-    def _(turn):
-        exchange(outward(turn), pieces, got, out_send, out_recv).start()
+    for offset in outward:
+        exchange(offset, pieces, got, out_send, out_recv).start()
 
     got[me] = pieces[me]
 
@@ -458,7 +454,7 @@
 
         def pair_step(i, p):
             return remote(
-                sent.at[i, p], other.at[i, p], pair_send, pair_recv.at[i, p], across
+                sent.at[i, p], other.at[i, p], pair_send, cross_recv.at[0, 2 * i + p], across
             )
 
         with jax.named_scope("last_sum"):
@@ -478,9 +474,11 @@
             distance = far - 2 if step == far else step
             distance = distance + late * hops
             ref = coef.at[slot(-ways[way] * distance), piece(i, p)]
-            return remote(
-                ref, ref, all_send, ring_recv.at[way, step, i, p], on_ring(hops * ways[way])
-            )
+            if step == far:
+                recv = cross_recv.at[1, TRI * way + i]
+            else:
+                recv = ring_recv.at[way, step, i, p]
+            return remote(ref, ref, all_send, recv, on_ring(hops * ways[way]))
 
         with jax.named_scope("pair"):
             for i in triples:
@@ -647,9 +645,8 @@
                 ]
                 back[2 * g + s] = jnp.concatenate(both, axis=0).astype(BF16)
 
-    @pl.loop(0, peers - 1)
-    def _(turn):
-        exchange(outward(turn), back, out, back_send, back_recv).start()
+    for offset in outward:
+        exchange(offset, back, out, back_send, back_recv).start()
 
     kept = pltpu.make_async_copy(back.at[me], out.at[me], own_sem)
     kept.start()
@@ -703,17 +700,15 @@
             vmem((ring, TRI * full, depth), BF16),
             vmem((2 * ring * full, LANES), F32),
             vmem(pieces, BF16),
-            dma((6,)),
-            dma,
-            dma,
-            dma,
-            dma,
-            dma,
-            dma,
-            dma,
-            dma,
-            dma((2, far + 1, TRI, 2)),
-            dma((TRI, 2)),
+            dma,
+            dma,
+            dma,
+            dma,
+            dma,
+            dma,
+            dma,
+            dma,
+            dma((2, far, TRI, 2)),
             dma((2, ring)),
             dma,
             dma,

time: 61.9 us -> 61.4 us (level)
  no operation moved by 1% of the time
where the time goes in v7:
time: 61.4 us; the launch traced here: 61.3 us
  Pallas kernels  61.3 us (100%)
    pallas_call x1, Pallas kernels, middle(): pl.pallas_call(functools.partial(middle_kernel, ring, cons), out_shape=ja...  57.8 us
    pallas_call x1, Pallas kernels, inverse(): pl.pallas_call(inverse_kernel, out_shape=jax.ShapeDtypeStruct((1, CYC, pe...  3.44 us

profile of v7, /device:TPU:1, one launch (start us, length us, event | category | flops | bytes accessed | tf_op | source)
XLA Modules:
  0.0 61.3 jit_solution(14984392049726054451)
XLA Ops:
  0.0 57.8 %middle.1.z_hbm = bf16[32,16,128]{2,1,0:T(8,128)(2,1)} custom-call(bf16[1,40,6144]{2,1,0:T(8,128)(2,1)} %elevation.1, bf16[40,48,768]{2,1,0:T(8,128)(2,1)} %legendre.1, f32[40]{0:T(128)} %cycle_weight.1, f32[768]{0:T(1024)} %love_factor.1, s32[16]{0:T(128)} %assigned.1, f32[96,128]{1,0:T(8,128)} %constant.4.clone.twiddles.twiddle_hbm, ...), custom_call_target="tpu_custom_call" | custom-call | tf_op jit(solution)/shard_map/middle/pallas_call | solution.py:672
  57.9 3.4 %inverse.1 = f32[1,40,6144]{2,1,0:T(8,128)} custom-call(bf16[32,16,128]{2,1,0:T(8,128)(2,1)} %middle.1.z_hbm, f32[96,128]{1,0:T(8,128)} %constant.4.clone.twiddles.twiddle_hbm, bf16[32,256]{1,0:T(8,128)(2,1)} %constant.5.clone.bases.basis_hbm), custom_call_target="tpu_custom_call" | custom-call | tf_op jit(solution)/shard_map/inverse/pallas_call | solution.py:203

commit v8 on v7

--- a/solution.py
+++ b/solution.py
@@ -54,8 +54,39 @@
     return half[index] if 2 * index <= length else conj(half[length - index])
 
 
+def minus(a, b):
+    return plus(a, negated(b))
+
+
+def negated(a):
+    return tuple(None if part is None else -part for part in a)
+
+
+def turned_left(a):
+    re, im = a
+    return None if im is None else -im, re
+
+
 def factor_of(length):
     return 4 if length % 4 == 0 else (3 if length % 3 == 0 else 2)
+
+
+def short_dft(values, sign):
+    n = len(values)
+    if n != 4:
+        out = []
+        for k in range(n):
+            total = values[0]
+            for i in range(1, n):
+                total = plus(total, by_phase(values[i], sign * i * k / n))
+            out.append(total)
+        return out
+    even, odd = plus(values[0], values[2]), plus(values[1], values[3])
+    even_gap, odd_gap = minus(values[0], values[2]), turned_left(minus(values[1], values[3]))
+    ahead, behind = plus(even_gap, odd_gap), minus(even_gap, odd_gap)
+    if sign < 0:
+        ahead, behind = behind, ahead
+    return [plus(even, odd), ahead, minus(even, odd), behind]
 
 
 def real_fft(values):
@@ -63,33 +94,43 @@
     if n == 1:
         return [(values[0], None)]
     p = factor_of(n)
+    short = n // p
     parts = [real_fft(values[i::p]) for i in range(p)]
-    out = []
-    for k in range(n // 2 + 1):
-        total = at(parts[0], k, n // p)
-        for i in range(1, p):
-            total = plus(total, by_phase(at(parts[i], k, n // p), -i * k / n))
-        out.append(total)
-    return out
+    out = [None] * n
+    for k in range(short):
+        if k > n // 2:
+            continue
+        spun = [by_phase(at(parts[i], k, short), -i * k / n) for i in range(p)]
+        for s, value in enumerate(short_dft(spun, -1)):
+            out[k + s * short] = value
+    half = out[: n // 2 + 1]
+    half[0] = (half[0][0], None)
+    if n % 2 == 0:
+        half[-1] = (half[-1][0], None)
+    return half
 
 
 def real_inverse(half, n):
     if n == 1:
         return [half[0][0]]
+    if n == 3:
+        base, (re, im) = half[0][0], half[1]
+        middle = base - re
+        side = im * np.float32(math.sqrt(3.0))
+        return [base + (re + re), middle - side, middle + side]
     p = factor_of(n)
     short = n // p
+    folded = [[None] * (short // 2 + 1) for _ in range(p)]
+    for r in range(short // 2 + 1):
+        mixed = short_dft([at(half, r + s * short, n) for s in range(p)], 1)
+        for a in range(p):
+            total = by_phase(mixed[a], r * a / n)
+            if r == 0 or 2 * r == short:
+                total = (total[0], None)
+            folded[a][r] = total
     out = [None] * n
     for a in range(p):
-        folded = []
-        for r in range(short // 2 + 1):
-            total = (None, None)
-            for s in range(p):
-                index = r + s * short
-                total = plus(total, by_phase(at(half, index, n), index * a / n))
-            if r == 0 or 2 * r == short:
-                total = (total[0], None)
-            folded.append(total)
-        for kk, value in enumerate(real_inverse(folded, short)):
+        for kk, value in enumerate(real_inverse(folded[a], short)):
             out[p * kk + a] = value
     return out
 
@@ -183,11 +224,11 @@
             cos, sin = twiddle_ref[2 * r : 2 * r + 1, :], twiddle_ref[2 * r + 1 : 2 * r + 2, :]
             turned.append((re * cos - im * sin, re * sin + im * cos))
         middle = RADIX // 2
-        half = [(turned[0][0], None)]
+        half = [(turned[0][0] + turned[0][0], None)]
         for r in range(1, middle):
             pair = plus(turned[r], conj(turned[RADIX - r]))
-            half.append((pair[0] * np.float32(0.5), pair[1] * np.float32(0.5)))
-        half.append((turned[middle][0], None))
+            half.append(pair)
+        half.append((turned[middle][0] + turned[middle][0], None))
         for k, value in enumerate(real_inverse(half, RADIX)):
             done[group, :, k * LANES : (k + 1) * LANES] = value
         leave(group).start()
@@ -200,6 +241,7 @@
 def inverse(pieces, period):
     cons = pieces.shape[0] // 2
     twiddle, basis = phase_tables(period)
+    twiddle = twiddle * np.float32(0.5)
     return pl.pallas_call(
         inverse_kernel,
         out_shape=jax.ShapeDtypeStruct((1, CYC, period), jnp.float32),
@@ -247,11 +289,15 @@
     full = 2 * cons
     barrier = pltpu.get_barrier_semaphore()
 
+    slots = {offset: lax.rem(z + offset + ring, ring) for offset in range(-far, far + 1)}
+    row_start = line * 2 * ring + core
+    near = {hops: (c, row_start + 2 * slots[hops]) for hops in (1, -1, 2, -2)}
+
     def slot(offset):
-        return lax.rem(z + offset + ring, ring)
+        return slots[offset]
 
     def on_ring(offset):
-        return (c, line * 2 * ring + slot(offset) * 2 + core)
+        return near[offset]
 
     outward = sorted(range(1, peers), key=lambda offset: abs(offset - peers // 2))
 
@@ -265,16 +311,25 @@
             device_id_type=MESH,
         )
 
+    def peer(offset):
+        if offset % 2:
+            return lax.rem(c + core + offset // 2, cons), 1 - core
+        return lax.rem(c + offset // 2, cons), core
+
     def exchange(offset, source, landing, send, recv):
-        index = lax.rem(me + offset, peers)
-        there = (index // 2, chip + lax.rem(index, 2))
-        return remote(source.at[index], landing.at[me], send, recv, there)
+        far_c, far_core = peer(offset)
+        there = (far_c, chip + far_core)
+        return remote(source.at[2 * far_c + far_core], landing.at[me], send, recv, there)
 
     def exchanged(source, landing, send, recv):
         rest = pl.ds(0, peers - 1)
         return remote(source.at[rest], landing.at[rest], send, recv, (c, chip + 1 - core))
 
     across = (c, (1 - line) * 2 * ring + z * 2 + core)
+    mine_rows = [pl.ds(pl.multiple_of(i * full + line * cons, cons), cons) for i in range(TRI)]
+    other_rows = [
+        pl.ds(pl.multiple_of(i * full + (1 - line) * cons, cons), cons) for i in range(TRI)
+    ]
 
     def half_of(which):
         return legendre.at[:, pl.ds(pl.multiple_of(which * half_orders, 8), half_orders), :]
@@ -297,8 +352,8 @@
             load.start()
 
         for offset in outward:
-            index = lax.rem(me + offset, peers)
-            there = (index // 2, chip + lax.rem(index, 2))
+            far_c, far_core = peer(offset)
+            there = (far_c, chip + far_core)
             pl.semaphore_signal(barrier, inc=1, device_id=there, device_id_type=MESH)
 
         for target in (on_ring(1), on_ring(-1), on_ring(2), on_ring(-2), across):
@@ -530,7 +585,7 @@
 
         def mixed_sum(owner, i):
             k = owners.index(owner)
-            return part[slot(owner), piece(i, line), :].astype(F32) + crossed[k, i].astype(F32)
+            return part[slot(owner), mine_rows[i], :].astype(F32) + crossed[k, i].astype(F32)
 
         def taken(owner, turn):
             k = owners.index(owner)
@@ -549,7 +604,7 @@
                 analysed(slot(owner))
                 for i in triples:
                     remote(
-                        part.at[slot(owner), piece(i, 1 - line)],
+                        part.at[slot(owner), other_rows[i]],
                         crossed.at[k, i],
                         pair_send,
                         cross_recv.at[0, k],
@@ -578,13 +633,13 @@
                             sum_step(way, step, i).start()
 
         def all_step(way, step, i, late=0):
-            ref = coef.at[slot(-ways[way] * (step + late)), piece(i, line)]
+            ref = coef.at[slot(-ways[way] * (step + late)), mine_rows[i]]
             return remote(
                 ref, ref, all_send, ring_recv.at[way, step, i, 0], on_ring(ways[way])
             )
 
         def shared(owner, i):
-            ref = coef.at[slot(owner), piece(i, line)]
+            ref = coef.at[slot(owner), mine_rows[i]]
             k = owners.index(owner)
             return remote(ref, ref, pair_send, cross_recv.at[1, k], across)
 
@@ -593,7 +648,7 @@
             for i in triples:
                 for way in ends:
                     sum_step(way, far - 1, i).wait_recv()
-                coef[z, piece(i, line), :] = (
+                coef[z, mine_rows[i], :] = (
                     (
                         mixed_sum(0, i)
                         + later[0, far - 2, i, 0].astype(F32)

time: 61.4 us -> 61.2 us (level)
  no operation moved by 1% of the time
where the time goes in v8:
time: 61.2 us; the launch traced here: 61 us
  Pallas kernels  61 us (100%)
    pallas_call x1, Pallas kernels, middle(): pl.pallas_call(functools.partial(middle_kernel, ring, cons), out_shape=ja...  58.1 us
    pallas_call x1, Pallas kernels, inverse(): pl.pallas_call(inverse_kernel, out_shape=jax.ShapeDtypeStruct((1, CYC, pe...  2.94 us

profile of v8, /device:TPU:1, one launch (start us, length us, event | category | flops | bytes accessed | tf_op | source)
XLA Modules:
  0.0 61.0 jit_solution(12402352607880711114)
XLA Ops:
  0.0 58.1 %middle.1.z_hbm = bf16[32,16,128]{2,1,0:T(8,128)(2,1)} custom-call(bf16[1,40,6144]{2,1,0:T(8,128)(2,1)} %elevation.1, bf16[40,48,768]{2,1,0:T(8,128)(2,1)} %legendre.1, f32[40]{0:T(128)} %cycle_weight.1, f32[768]{0:T(1024)} %love_factor.1, s32[16]{0:T(128)} %assigned.1, f32[96,128]{1,0:T(8,128)} %constant.6.clone.twiddles, ...), custom_call_target="tpu_custom_call" | custom-call | tf_op jit(solution)/shard_map/middle/pallas_call | solution.py:727
  58.1 2.9 %inverse.1 = f32[1,40,6144]{2,1,0:T(8,128)} custom-call(bf16[32,16,128]{2,1,0:T(8,128)(2,1)} %middle.1.z_hbm, f32[96,128]{1,0:T(8,128)} %constant.8.clone.twiddle_hbm, bf16[32,256]{1,0:T(8,128)(2,1)} %constant.7.clone.bases.basis_hbm), custom_call_target="tpu_custom_call" | custom-call | tf_op jit(solution)/shard_map/inverse/pallas_call | solution.py:245

commit v9 on v8

--- a/solution.py
+++ b/solution.py
@@ -478,12 +478,13 @@
 
         with jax.named_scope("first_part"):
             analysed(slot(far))
-            for i in triples:
-                for way in ends:
-                    sum_step(way, 0, i, way).start()
+            for way in ends:
+                sum_step(way, 0, 0, way).start()
             for way in ends:
                 analysed(slot(ways[way] * (far - 1)))
                 for i in triples:
+                    if i:
+                        sum_step(way, 0, i, way).start()
                     for p in (1 - way, way):
                         sum_step(way, 1, i, p).start()
             for step in range(2, far):
@@ -550,9 +551,9 @@
                     for p in ends:
                         for way in ends:
                             all_step(way, step - 1, i, p, 1).wait_recv()
-                            all_step(way, step, i, p).start()
                             if step == far - 2 and p == way:
                                 all_step(way, far, i, p).start()
+                            all_step(way, step, i, p).start()
             with jax.named_scope(f"synth#s={step}"):
                 for owner in (0,) if step == 1 else (step - 1, 1 - step):
                     synthesised(slot(owner))
@@ -633,10 +634,11 @@
                             sum_step(way, step, i).start()
 
         def all_step(way, step, i, late=0):
-            ref = coef.at[slot(-ways[way] * (step + late)), mine_rows[i]]
-            return remote(
-                ref, ref, all_send, ring_recv.at[way, step, i, 0], on_ring(ways[way])
-            )
+            direct = int(step == far - 1)
+            distance = step - direct + late * (1 + direct)
+            ref = coef.at[slot(-ways[way] * distance), mine_rows[i]]
+            recv = ring_recv.at[way, step, i, direct]
+            return remote(ref, ref, all_send, recv, on_ring((1 + direct) * ways[way]))
 
         def shared(owner, i):
             ref = coef.at[slot(owner), mine_rows[i]]
@@ -669,7 +671,9 @@
                 for i in triples:
                     for way in ends:
                         all_step(way, step - 1, i, 1).wait_recv()
-                        if step < far - 1 or way == i % 2:
+                        if step == far - 2 and way == i % 2:
+                            all_step(way, far - 1, i).start()
+                        if step < far - 1:
                             all_step(way, step, i).start()
                         shared(-ways[way] * step, i).start()
             with jax.named_scope(f"synth#s={step}"):

time: 61.2 us -> 60.5 us (0.989)
  Pallas kernels: 61 us -> 60.3 us
    pallas_call x1, Pallas kernels: 58.1 us -> 57.4 us  [middle(): pl.pallas_call(functools.partial(middle_kernel, ring, cons), out_shape=ja...]
where the time goes in v9:
time: 60.5 us; the launch traced here: 60.4 us
  Pallas kernels  60.3 us (100%)
    pallas_call x1, Pallas kernels, middle(): pl.pallas_call(functools.partial(middle_kernel, ring, cons), out_shape=ja...  57.4 us
    pallas_call x1, Pallas kernels, inverse(): pl.pallas_call(inverse_kernel, out_shape=jax.ShapeDtypeStruct((1, CYC, pe...  2.93 us

profile of v9, /device:TPU:1, one launch (start us, length us, event | category | flops | bytes accessed | tf_op | source)
XLA Modules:
  0.0 60.4 jit_solution(2250849597248680365)
XLA Ops:
  0.0 57.4 %middle.1.z_hbm = bf16[32,16,128]{2,1,0:T(8,128)(2,1)} custom-call(bf16[1,40,6144]{2,1,0:T(8,128)(2,1)} %elevation.1, bf16[40,48,768]{2,1,0:T(8,128)(2,1)} %legendre.1, f32[40]{0:T(128)} %cycle_weight.1, f32[768]{0:T(1024)} %love_factor.1, s32[16]{0:T(128)} %assigned.1, f32[96,128]{1,0:T(8,128)} %constant.6.clone.twiddles, ...), custom_call_target="tpu_custom_call" | custom-call | tf_op jit(solution)/shard_map/middle/pallas_call | solution.py:731
  57.4 2.9 %inverse.1 = f32[1,40,6144]{2,1,0:T(8,128)} custom-call(bf16[32,16,128]{2,1,0:T(8,128)(2,1)} %middle.1.z_hbm, f32[96,128]{1,0:T(8,128)} %constant.8.clone.twiddle_hbm, bf16[32,256]{1,0:T(8,128)(2,1)} %constant.7.clone.bases.basis_hbm), custom_call_target="tpu_custom_call" | custom-call | tf_op jit(solution)/shard_map/inverse/pallas_call | solution.py:245

commit v10 on v9

--- a/solution.py
+++ b/solution.py
@@ -327,9 +327,6 @@
 
     across = (c, (1 - line) * 2 * ring + z * 2 + core)
     mine_rows = [pl.ds(pl.multiple_of(i * full + line * cons, cons), cons) for i in range(TRI)]
-    other_rows = [
-        pl.ds(pl.multiple_of(i * full + (1 - line) * cons, cons), cons) for i in range(TRI)
-    ]
 
     def half_of(which):
         return legendre.at[:, pl.ds(pl.multiple_of(which * half_orders, 8), half_orders), :]
@@ -433,9 +430,10 @@
     def analysed(t):
         x = lines[t]
         left = [jnp.where(which == i, x, 0.0) for i in range(TRI)]
-        part[t] = jnp.dot(
+        made = jnp.dot(
             jnp.concatenate(left, axis=0).astype(BF16), table[t], preferred_element_type=F32
-        ).astype(BF16)
+        )
+        part[t] = made.astype(BF16).reshape(TRI, 2, cons, depth)
 
     def piece(i, p):
         return pl.ds(pl.multiple_of(i * full + p * cons, cons), cons)
@@ -467,11 +465,11 @@
     def _():
         def sum_step(way, step, i, p):
             if step == 0:
-                source = part.at[slot(far), piece(i, p)]
+                source = part.at[slot(far), i, p]
                 return sum_sent(source, first.at[way, i], way, step, i, p, 2)
             target = later.at[way, step - 1, i, p]
             if step == 1:
-                source = part.at[slot(ways[way] * (far - 1)), piece(i, p)]
+                source = part.at[slot(ways[way] * (far - 1)), i, p]
             else:
                 source = staged.at[way, step - 1, i, p]
             return sum_sent(source, target, way, step, i, p)
@@ -499,7 +497,7 @@
                             p = way if late else 1 - way
                             owner = slot(ways[way] * (far - step))
                             sum_step(way, step - 1, i, p).wait_recv()
-                            total = part[owner, piece(i, p), :].astype(F32) + later[
+                            total = part[owner, i, p].astype(F32) + later[
                                 way, step - 2, i, p
                             ].astype(F32)
                             if step == 2 and late:
@@ -519,7 +517,7 @@
                     for way in ends:
                         sum_step(way, far - 1, i, p).wait_recv()
                     sent[i, p] = (
-                        part[z, piece(i, p), :].astype(F32)
+                        part[z, i, p].astype(F32)
                         + later[0, far - 2, i, p].astype(F32)
                         + later[1, far - 2, i, p].astype(F32)
                     ).astype(BF16)
@@ -586,7 +584,7 @@
 
         def mixed_sum(owner, i):
             k = owners.index(owner)
-            return part[slot(owner), mine_rows[i], :].astype(F32) + crossed[k, i].astype(F32)
+            return part[slot(owner), i, line].astype(F32) + crossed[k, i].astype(F32)
 
         def taken(owner, turn):
             k = owners.index(owner)
@@ -603,14 +601,13 @@
         with jax.named_scope("first_part"):
             for k, owner in enumerate(owners):
                 analysed(slot(owner))
-                for i in triples:
-                    remote(
-                        part.at[slot(owner), other_rows[i]],
-                        crossed.at[k, i],
-                        pair_send,
-                        cross_recv.at[0, k],
-                        across,
-                    ).start()
+                remote(
+                    part.at[slot(owner), :, 1 - line],
+                    crossed.at[k],
+                    pair_send,
+                    cross_recv.at[0, k],
+                    across,
+                ).start()
         with jax.named_scope("sum#s=0"):
             taken(far, 0)
             for i in triples:
@@ -749,7 +746,7 @@
             vmem(pieces, BF16),
             vmem((2 * cons * 16, LANES), F32),
             vmem((ring, full, 2 * LANES), F32),
-            vmem((ring, TRI * full, depth), BF16),
+            vmem((ring, TRI, 2, cons, depth), BF16),
             vmem((2, TRI, cons, depth), BF16),
             vmem((2, far - 1, TRI, 2, cons, depth), BF16),
             vmem((2, far - 1, TRI, 2, cons, depth), BF16),

time: 60.5 us -> 60.5 us (level)
  no operation moved by 1% of the time
where the time goes in v10:
time: 60.5 us; the launch traced here: 60.3 us
  Pallas kernels  60.3 us (100%)
    pallas_call x1, Pallas kernels, middle(): pl.pallas_call(functools.partial(middle_kernel, ring, cons), out_shape=ja...  57.4 us
    pallas_call x1, Pallas kernels, inverse(): pl.pallas_call(inverse_kernel, out_shape=jax.ShapeDtypeStruct((1, CYC, pe...  2.94 us

profile of v10, /device:TPU:1, one launch (start us, length us, event | category | flops | bytes accessed | tf_op | source)
XLA Modules:
  0.0 60.3 jit_solution(5320001043895705427)
XLA Ops:
  0.0 57.4 %middle.1.z_hbm = bf16[32,16,128]{2,1,0:T(8,128)(2,1)} custom-call(bf16[1,40,6144]{2,1,0:T(8,128)(2,1)} %elevation.1, bf16[40,48,768]{2,1,0:T(8,128)(2,1)} %legendre.1, f32[40]{0:T(128)} %cycle_weight.1, f32[768]{0:T(1024)} %love_factor.1, s32[16]{0:T(128)} %assigned.1, f32[96,128]{1,0:T(8,128)} %constant.6.clone.twiddles, ...), custom_call_target="tpu_custom_call" | custom-call | tf_op jit(solution)/shard_map/middle/pallas_call | solution.py:728
  57.4 2.9 %inverse.1 = f32[1,40,6144]{2,1,0:T(8,128)} custom-call(bf16[32,16,128]{2,1,0:T(8,128)(2,1)} %middle.1.z_hbm, f32[96,128]{1,0:T(8,128)} %constant.8.clone.twiddle_hbm, bf16[32,256]{1,0:T(8,128)(2,1)} %constant.7.clone.bases.basis_hbm), custom_call_target="tpu_custom_call" | custom-call | tf_op jit(solution)/shard_map/inverse/pallas_call | solution.py:245
